TPU v7x, 32 devices: a whole 2x2x4 slice. The times are simulated.
32 devices in a mesh: img: 2 (over core), band: 4 (over z), pw: 4 (over y, x).
Axes of the slice: x: 2, y: 2, z: 4, core: 2. Of those that a mesh axis runs over, the one named last changes fastest.
Arguments:
- coefficients: bfloat16 [2, 1024, 32, 2048], P('img', None, ('band', 'pw')), may hold values from -6 to 6
- rotation: bfloat16 [2, 1024, 256], P('img'), may hold values from -0.1875 to 0.1875
- positions: int32 [2, 3, 256], P('img'), may hold values from 0 to 63, as said below
- start_pos: int32 [3, 256], replicated, may hold values from 0 to 63, as said below
- end_pos: int32 [3, 256], replicated, may hold values from 0 to 63, as said below
- species: int32 [256], replicated, may hold values from 0 to 3
- depth: float32 [4], replicated, may hold values from 0.5 to 3
Outputs:
- correction: bfloat16 [2, 256, 32, 2048], P('img', None, ('band', 'pw'))
- ritz_values: float32 [2, 256], P('img')
- band_force: float32 [2, 3, 256], P('img')
- along_force: float32 [2], P('img')
Inputs may be any that keep to these rules, and one draw needn't show every extreme that they name: `positions`: grid index of each atom's centre along each dimension. `start_pos`: grid index of each atom's centre along each dimension. `end_pos`: grid index of each atom's centre along each dimension.
All inputs are finite; a program needn't handle non-finite values.
Results may differ from a plain program's by a relative error of at most 0.012.
The roundings to bfloat16 on the way count: a program that leaves them out, or rounds other values in their place, can miss the bound.
Values may be sent and summed in bfloat16 or wider, within the bound.
A program may use at most 128 MiB of HBM per device.

v0:
```python
import math

import jax
import jax.numpy as jnp
import numpy as np
from jax import lax
from jax.experimental import pallas as pl
from jax.experimental.pallas import tpu as pltpu
from jax.sharding import PartitionSpec as P

G = 64
W = 32
BANDS = 1024
BLOCK = 256
SPECIES = 4


kinetic_scale = 0.01
sigma_cells = 3.0
spring_constant = 2.0
epsilon = 1e-06
highest = lax.Precision.HIGHEST


def passed_along(block, axis, distance):
    devices = range(lax.axis_size(axis))
    route = [(i - distance, i) for i in devices if i - distance in devices]
    return lax.ppermute(block, axis, route)


def phases():
    wavenum = np.arange(W, dtype=np.int32) - W // 2
    grid_cells = np.arange(G, dtype=np.int32)
    turn_count = np.mod(wavenum[:, None] * grid_cells[None, :], G)
    return turn_count.astype(np.float32) * np.float32(2.0 * math.pi / G)


def forward_table():
    angle_tab = phases()
    cosine = np.cos(angle_tab) / np.float32(math.sqrt(W))
    sine_part = np.sin(angle_tab) / np.float32(math.sqrt(W))
    return np.stack([np.stack([cosine, sine_part], 1), np.stack([-sine_part, cosine], 1)], 0)


def inverse_table():
    angle_tab = phases().T
    factor = np.float32(math.sqrt(W) / G)
    cosine = np.cos(angle_tab) * factor
    sine_part = np.sin(angle_tab) * factor
    return np.stack([np.stack([cosine, -sine_part], 1), np.stack([sine_part, cosine], 1)], 0)


def kernel_tables():
    fwd = forward_table()
    inv = inverse_table()
    two = np.eye(2, dtype=np.float32)
    table_z = np.einsum("czdn,vw,ij->jviczdwn", fwd, two, two).reshape(2, 8 * W, 4 * G)
    back_z = np.einsum("dncz,vw,ij->jdwnvicz", inv, two, two).reshape(2, 4 * G, 8 * W)
    fwd_y = fwd.reshape(2, W // 2, 2, 2, G)
    table_y = np.einsum("dgpem->empdg", fwd_y).reshape(2 * G, 2 * W)
    table_x = np.einsum("dxem->emxd", fwd).reshape(2 * G, 2 * W)
    back_x = np.einsum("emdx->xdem", inv).reshape(2 * W, 2 * G)
    inv_y = inv.reshape(2, G, 2, W // 2, 2)
    back_y = np.einsum("dmcgp->pcgdm", inv_y).reshape(2 * W, 2 * G)
    listed = (table_z, table_y, table_x, back_x, back_y, back_z)
    return [jnp.asarray(t, dtype=jnp.bfloat16) for t in listed]


def kinetic_table():
    wave = np.arange(W, dtype=np.int32) - W // 2
    sq = wave * wave
    squared = sq[:, None, None, None] + sq[None, :, None, None] + sq[None, None, None, :]
    squared = np.broadcast_to(squared, (W, W, 2, W)).reshape(W * W // 2, 4 * W)
    return np.float32(kinetic_scale * 0.5) * squared.astype(np.float32)


def mm(left, right):
    return jnp.dot(left, right, preferred_element_type=jnp.float32)


def apply_kernel(
    vec_ref, pot_ref, kin_ref, tz_ref, ty_ref, tx_ref, bx_ref, by_ref, bz_ref,
    out_ref, ritz_ref, dens_ref, zs_ref, s_ref,
):
    lanes = 2 * G
    half = W // 2
    rows = W * half
    bf = jnp.bfloat16

    @pl.when(pl.program_id(0) == 0)
    def _():
        dens_ref[...] = jnp.zeros_like(dens_ref)

    def pair_in():
        return jnp.concatenate(
            [vec_ref[:, v].reshape(rows, 4 * W) for v in range(2)], axis=1
        )

    vecs = pair_in()
    for p in range(2):
        zs_ref[p] = mm(vecs, tz_ref[p]).astype(bf)

    def y_step(i, carry):
        cols = []
        for k in range(2):
            at = pl.ds(pl.multiple_of((2 * i + k) * half, half), half)
            parts = [zs_ref[p, at, d * lanes : (d + 1) * lanes] for p in range(2) for d in range(2)]
            cols.append(jnp.concatenate(parts, axis=0))
        done = mm(ty_ref[...], jnp.concatenate(cols, axis=1))
        for k in range(2):
            at = pl.ds(pl.multiple_of((2 * i + k) * lanes, lanes), lanes)
            s_ref[at, :] = done[:, k * lanes : (k + 1) * lanes]
        return carry

    lax.fori_loop(0, W // 2, y_step, 0, unroll=4)

    def x_step(i, carry):
        ats = [pl.ds(2 * i + k, 2 * W, stride=G) for k in range(2)]
        cols = [s_ref[at, :].astype(bf) for at in ats]
        done = mm(tx_ref[...], jnp.concatenate(cols, axis=1))
        real, imag = (done[:G], done[G:])
        pot = jnp.concatenate([pot_ref[2 * i], pot_ref[2 * i + 1]], axis=1)
        square = real * real + imag * imag
        for k in range(2):
            dens_ref[2 * i + k] += square[:, k * lanes : (k + 1) * lanes]
        weighted = jnp.concatenate([(real * pot).astype(bf), (imag * pot).astype(bf)], axis=0)
        back = mm(bx_ref[...], weighted)
        for k in range(2):
            s_ref[ats[k], :] = back[:, k * lanes : (k + 1) * lanes]
        return carry

    lax.fori_loop(0, G // 2, x_step, 0, unroll=4)

    def back_y_step(i, carry):
        cols = []
        for k in range(2):
            at = pl.ds(pl.multiple_of((2 * i + k) * lanes, lanes), lanes)
            cols.append(s_ref[at, :].astype(bf))
        done = mm(by_ref[...], jnp.concatenate(cols, axis=1)).astype(bf)
        for k in range(2):
            at = pl.ds(pl.multiple_of((2 * i + k) * half, half), half)
            for p in range(2):
                for c in range(2):
                    r = (2 * p + c) * half
                    zs_ref[p, at, c * lanes : (c + 1) * lanes] = done[
                        r : r + half, k * lanes : (k + 1) * lanes
                    ]
        return carry

    lax.fori_loop(0, W // 2, back_y_step, 0, unroll=4)

    local = mm(zs_ref[0], bz_ref[0]) + mm(zs_ref[1], bz_ref[1])
    kin = kin_ref[...]
    npw_total = W * W * W
    for v in range(2):
        orb = vec_ref[:, v].reshape(rows, 4 * W).astype(jnp.float32)
        ham = kin * orb + local[:, v * 4 * W : (v + 1) * 4 * W]
        numerator = jnp.sum(jnp.sum(orb * ham, axis=0, keepdims=True), axis=1, keepdims=True)
        denominator = jnp.sum(jnp.sum(orb * orb, axis=0, keepdims=True), axis=1, keepdims=True)
        ritz = numerator / npw_total / (denominator / npw_total + epsilon)
        search = ((ham - ritz * orb) / (1.0 + kin)).astype(bf)
        out_ref[:, v] = search.reshape(vec_ref.shape[0], *vec_ref.shape[2:])
        ritz_ref[0, :, v * 128 : (v + 1) * 128] = jnp.broadcast_to(ritz, (8, 128))


def apply_local(whole, potential):
    devices, vectors, planes, half, lanes = whole.shape
    tabs = kernel_tables()
    kin = jnp.asarray(kinetic_table())
    block = (devices, 2, planes, half, lanes)

    def fixed(arr):
        return pl.BlockSpec(arr.shape, lambda p, n=arr.ndim: (0,) * n)

    flops = vectors * 2 * 2 * (W * W * 2 * W * 2 * G + W * G * 2 * W * 2 * G + G * G * 2 * W * 2 * G)
    return pl.pallas_call(
        apply_kernel,
        grid=(vectors // 2,),
        in_specs=[pl.BlockSpec(block, lambda p: (0, p, 0, 0, 0)), fixed(potential), fixed(kin)]
        + [fixed(t) for t in tabs],
        out_specs=[
            pl.BlockSpec(block, lambda p: (0, p, 0, 0, 0)),
            pl.BlockSpec((1, 8, 256), lambda p: (p, 0, 0)),
            pl.BlockSpec((G, G, 2 * G), lambda p: (0, 0, 0)),
        ],
        out_shape=[
            jax.ShapeDtypeStruct(whole.shape, jnp.bfloat16),
            jax.ShapeDtypeStruct((vectors // 2, 8, 256), jnp.float32),
            jax.ShapeDtypeStruct((G, G, 2 * G), jnp.float32),
        ],
        scratch_shapes=[
            pltpu.VMEM((2, W * W // 2, 4 * G), jnp.bfloat16),
            pltpu.VMEM((W * 2 * G, 2 * G), jnp.float32),
        ],
        compiler_params=pltpu.CompilerParams(
            dimension_semantics=("arbitrary",), vmem_limit_bytes=48 * 1024 * 1024
        ),
        cost_estimate=pl.CostEstimate(flops=flops, bytes_accessed=8 << 20, transcendentals=0),
        name="apply_local",
    )(whole, potential, kin, *tabs)


def turn_kernel(c_ref, r_ref, out_ref):
    block = c_ref[...]
    out_ref[0] = block
    size = r_ref.shape[0]
    for t in range(block.shape[1] // size):
        at = slice(t * size, (t + 1) * size)
        out_ref[1, :, at] = mm(block[:, at], r_ref[...]).astype(jnp.bfloat16)


def with_turned(flat_all):
    bands, entries = flat_all.shape
    one = np.zeros((2, W, 2, W), np.float32)
    one[1, :, 0, :] = -np.eye(W)
    one[0, :, 1, :] = np.eye(W)
    turn = np.kron(np.eye(4, dtype=np.float32), one.reshape(2 * W, 2 * W))
    turn = jnp.asarray(turn, dtype=jnp.bfloat16)
    tile = 256
    return pl.pallas_call(
        turn_kernel,
        grid=(bands // tile,),
        in_specs=[
            pl.BlockSpec((tile, entries), lambda p: (p, 0)),
            pl.BlockSpec(turn.shape, lambda p: (0, 0)),
        ],
        out_specs=pl.BlockSpec((2, tile, entries), lambda p: (0, p, 0)),
        out_shape=jax.ShapeDtypeStruct((2, bands, entries), jnp.bfloat16),
        compiler_params=pltpu.CompilerParams(
            dimension_semantics=("arbitrary",), vmem_limit_bytes=40 * 1024 * 1024
        ),
        cost_estimate=pl.CostEstimate(
            flops=2 * bands * entries * 256, bytes_accessed=6 * bands * entries, transcendentals=0
        ),
        name="with_turned",
    )(flat_all, turn)


def wrap_offset(values):
    return jnp.mod(values + G // 2, G) - G // 2


def gaussians(coords, grid_cells):
    offset = wrap_offset(grid_cells[None, :] - coords[:, None]).astype(jnp.float32)
    return (jnp.exp(-offset * offset / (2.0 * sigma_cells * sigma_cells)), offset)


def atom_tables(own_pos, y_cells):
    grid_cells = jnp.arange(G, dtype=jnp.int32)
    gauss_x, offset_x = gaussians(own_pos[0], grid_cells)
    gauss_y, offset_y = gaussians(own_pos[1], y_cells)
    gauss_z, offset_z = gaussians(own_pos[2], grid_cells)
    return (gauss_x, offset_x, gauss_y, offset_y, gauss_z, offset_z)


def local_potential(tables, strength):
    gauss_x, offset_x, gauss_y, offset_y, gauss_z, offset_z = tables
    atom_count = gauss_x.shape[0]
    joined = (gauss_y[:, :, None] * gauss_z[:, None, :]).reshape(atom_count, -1)
    potential = jnp.dot((strength[:, None] * gauss_x).T, joined, precision=highest)
    return (potential, joined)


def atom_forces(density, tables, joined, strength):
    gauss_x, offset_x, gauss_y, offset_y, gauss_z, offset_z = tables
    atom_count = gauss_x.shape[0]
    with_y = ((gauss_y * offset_y)[:, :, None] * gauss_z[:, None, :]).reshape(atom_count, -1)
    with_z = (gauss_y[:, :, None] * (gauss_z * offset_z)[:, None, :]).reshape(atom_count, -1)
    stacked = jnp.concatenate([joined, with_y, with_z], 0)
    moments = jnp.dot(density, stacked.T, precision=highest)
    prefactor = -strength / (sigma_cells * sigma_cells)
    force_x = prefactor * jnp.sum(gauss_x * offset_x * moments[:, :atom_count].T, 1)
    force_y = prefactor * jnp.sum(gauss_x * moments[:, atom_count : 2 * atom_count].T, 1)
    force_z = prefactor * jnp.sum(gauss_x * moments[:, 2 * atom_count :].T, 1)
    return jnp.stack([force_x, force_y, force_z], 0)


def chain_forces(force, own_pos, before, after):
    ahead_step = wrap_offset(after - own_pos).astype(jnp.float32)
    behind = wrap_offset(own_pos - before).astype(jnp.float32)
    tangent_raw = ahead_step + behind
    entries = 3 * own_pos.shape[1]
    tangent = (
        tangent_raw * lax.rsqrt(jnp.mean(tangent_raw * tangent_raw) + epsilon) / math.sqrt(entries)
    )
    length_ahead = jnp.sqrt(entries * (jnp.mean(ahead_step * ahead_step) + epsilon))
    length_behind = jnp.sqrt(entries * (jnp.mean(behind * behind) + epsilon))
    along_path = jnp.sum(force * tangent)
    band_push = (
        force - along_path * tangent + spring_constant * (length_ahead - length_behind) * tangent
    )
    return (band_push, along_path)


def body(coefficients, rotation, positions, start_pos, end_pos, species, depth):
    axes = ("band", "pw")
    devices = lax.axis_size(axes)
    coeff_all = coefficients[0]
    planes = coeff_all.shape[1]
    flat_all = coeff_all.reshape(BANDS, -1)
    vectors = BLOCK // devices
    orbitals = jnp.einsum("ib,ik->bk", rotation[0], flat_all, preferred_element_type=jnp.float32)
    orbitals = orbitals.astype(jnp.bfloat16).reshape(BLOCK, planes * (W // 2), 4 * W)
    whole = lax.all_to_all(orbitals, axes, split_axis=0, concat_axis=0, tiled=True)
    whole = whole.reshape(devices, vectors, planes, W // 2, 4 * W)
    both = with_turned(flat_all)
    kind_ids = jnp.arange(SPECIES, dtype=jnp.int32)
    strength = jnp.sum(jnp.where(species[:, None] == kind_ids[None, :], depth[None, :], 0.0), 1)
    own_pos = positions[0]
    tables = atom_tables(own_pos, jnp.arange(G, dtype=jnp.int32))
    potential, joined = local_potential(tables, strength)
    potential = jnp.swapaxes(potential.reshape(G, G, G), 0, 1)
    potential = jnp.concatenate([potential, potential], 2)
    search, ritz, density = apply_local(whole, potential)
    search = search.reshape(BLOCK, planes * (W // 2), 4 * W)
    search = lax.all_to_all(search, axes, split_axis=0, concat_axis=0, tiled=True)
    search = search.reshape(BLOCK, -1)
    density = jnp.swapaxes(density[:, :, :G] + density[:, :, G:], 0, 1).reshape(G, G * G) / BLOCK
    force_part = atom_forces(density, tables, joined, strength)
    own_ritz = ritz[:, 0, ::128].reshape(vectors)
    ritz_part = lax.dynamic_update_slice(
        jnp.zeros((BLOCK,), jnp.float32), own_ritz, (lax.axis_index(axes) * vectors,)
    )
    summed = lax.psum(jnp.concatenate([force_part.reshape(-1), ritz_part]), axes)
    atom_force = summed[: force_part.size].reshape(force_part.shape)
    ritz_values = summed[force_part.size :]
    npw_total = W * W * W
    stacked = both.reshape(2 * BANDS, -1)
    partial = jnp.einsum("ik,jk->ij", stacked, search, preferred_element_type=jnp.float32)
    partial = (partial / npw_total).astype(jnp.bfloat16)
    arrived = lax.all_to_all(partial, axes, split_axis=0, concat_axis=0, tiled=True)
    arrived = arrived.reshape(devices, 2 * BANDS // devices, BLOCK).astype(jnp.float32)
    own_sum = jnp.sum(arrived, 0).astype(jnp.bfloat16)
    intersections = lax.all_gather(own_sum, axes, axis=0, tiled=True)
    projection = jnp.einsum(
        "ij,ik->jk", intersections, stacked, preferred_element_type=jnp.float32
    )
    correction = (search.astype(jnp.float32) - projection).astype(jnp.bfloat16)
    correction = correction.reshape(BLOCK, planes, W * 2 * W)
    image_idx = lax.axis_index("img")
    before = passed_along(own_pos, "img", 1)
    after = passed_along(own_pos, "img", -1)
    before = jnp.where(image_idx == 0, start_pos, before)
    after = jnp.where(image_idx == lax.axis_size("img") - 1, end_pos, after)
    band_push, along_path = chain_forces(atom_force, own_pos, before, after)
    return (correction[None], ritz_values[None], band_push[None], along_path[None])


def solution(mesh):
    in_specs = (
        P("img", None, ("band", "pw"), None),
        P("img", None, None),
        P("img", None, None),
        P(),
        P(),
        P(),
        P(),
    )
    out_specs = (
        P("img", None, ("band", "pw"), None),
        P("img", None),
        P("img", None, None),
        P("img"),
    )
    return jax.shard_map(body, mesh=mesh, in_specs=in_specs, out_specs=out_specs, check_vma=False)
```

profile of v0, /device:TPU:0, one launch (start us, length us, event | category | flops | bytes accessed | tf_op | source)
XLA Modules:
  0.0 348.9 jit_solution(7843742474262476894)
XLA Ops:
  7.2 0.0 copy-start
  7.2 12.1 %copy.22 = bf16[128,8,2,2048]{3,1,2,0:T(8,128)(2,1)} copy(bf16[128,8,2,2048]{3,2,1,0:T(2,128)(2,1)} %bitcast.82) | data formatting | bytes 16777216
  19.2 5.8 %fusion.15 = bf16[32,8,32,128]{3,1,2,0:T(8,128)(2,1)S(1)} fusion(bf16[1024,4096]{1,0:T(8,128)(2,1)} %bitcast.77, bf16[1,1024,256]{2,1,0:T(8,128)(2,1)S(1)} %copy-done), kind=kOutput, calls=%fused_computation.21 | convolution fusion | flops 2148532224 | bytes 11010048 | tf_op jit(solution)/shard_map/ib,ik->bk/dot_general | solution.py:302
  25.1 1.8 copy.23
  26.9 8.5 %all-to-all-start = ((bf16[256,32,128]{2,1,0:T(8,128)(2,1)}), bf16[256,32,128]{2,1,0:T(8,128)(2,1)S(1)}, u32[]{:S(2)}, u32[]{:S(2)}) async-start(bf16[256,32,128]{2,1,0:T(8,128)(2,1)} %bitcast.31), calls=%async_computation | async-start | bytes 4194304 | tf_op jit(solution)/shard_map/all_to_all | solution.py:304
  35.4 0.0 copy-start.5
  35.4 0.0 copy-start.6
  35.4 0.0 copy-start.7
  35.4 0.0 copy-start.8
  35.5 0.1 select_reduce_fusion
  35.6 0.1 fusion.41
  35.7 6.1 %fusion.12 = f32[64,64,64]{2,1,0:T(8,128)S(1)} fusion(f32[256,64]{0,1:T(8,128)S(1)} %get-tuple-element.29, f32[256,64]{0,1:T(8,128)S(1)} %get-tuple-element.30, s32[256]{0:T(256)S(1)} %bitcast.89, f32[256]{0:T(256)S(1)} %select_reduce_fusion), kind=kOutput, calls=%fused_computation.20 | convolution fusion | flops 806666240 | bytes 1181696 | tf_op jit(solution)/shard_map/dot_general | solution.py:260
  41.8 2.0 pad_maximum_fusion.pot_ref
  43.8 34.6 %all-to-all-done = bf16[256,32,128]{2,1,0:T(8,128)(2,1)S(1)} async-done(((bf16[256,32,128]{2,1,0:T(8,128)(2,1)}), bf16[256,32,128]{2,1,0:T(8,128)(2,1)S(1)}, u32[]{:S(2)}, u32[]{:S(2)}) %all-to-all-start) | async-done | bytes 2097184 | tf_op jit(solution)/shard_map/all_to_all | solution.py:304
  78.4 1.3 copy-done.12
  79.7 80.3 %apply_local.1 = (bf16[16,16,2,16,128]{4,3,2,1,0:T(8,128)(2,1)S(1)}, f32[8,8,256]{2,1,0:T(8,128)S(1)}, f32[64,64,128]{2,1,0:T(8,128)S(1)}) custom-call(bf16[16,16,2,16,128]{4,3,2,1,0:T(8,128)(2,1)} %bitcast.86, f32[64,64,128]{2,1,0:T(8,128)} %pad_maximum_fusion.pot_ref, f32[512,128]{1,0:T(8,128)S(1)} %copy-done.5, bf16[2,256,256]{2,1,0:T(8,128)(2,1)S(1)} %copy-done.6, ...), custom_call_target="tpu_custom_call" | custom-call | flops 3758096384 | bytes 8388608 | tf_op jit(solution)/shard_map/apply_local/pallas_call | solution.py:176
  160.0 1.3 copy-done.3
  161.3 10.2 %all-to-all-start.1 = ((bf16[256,32,128]{2,1,0:T(8,128)(2,1)}), bf16[256,32,128]{2,1,0:T(8,128)(2,1)}, u32[]{:S(2)}, u32[]{:S(2)}) async-start(bf16[256,32,128]{2,1,0:T(8,128)(2,1)} %bitcast.79), calls=%async_computation.1 | async-start | bytes 4194304 | tf_op jit(solution)/shard_map/all_to_all | solution.py:316
  171.6 3.4 copy-done.2
  174.9 6.6 %with_turned.1 = bf16[2,1024,4096]{2,1,0:T(8,128)(2,1)} custom-call(bf16[1024,4096]{1,0:T(8,128)(2,1)S(1)} %bitcast.78, bf16[256,256]{1,0:T(8,128)(2,1)S(1)} %copy-done.4), custom_call_target="tpu_custom_call" | custom-call | flops 2147483648 | bytes 25165824 | tf_op jit(solution)/shard_map/with_turned/pallas_call | solution.py:220
  181.5 32.5 %all-to-all-done.1 = bf16[256,32,128]{2,1,0:T(8,128)(2,1)} async-done(((bf16[256,32,128]{2,1,0:T(8,128)(2,1)}), bf16[256,32,128]{2,1,0:T(8,128)(2,1)}, u32[]{:S(2)}, u32[]{:S(2)}) %all-to-all-start.1) | async-done | bytes 2097184 | tf_op jit(solution)/shard_map/all_to_all | solution.py:316
  214.1 12.1 %fusion.9 = bf16[2048,256]{1,0:T(8,128)(2,1)} fusion(bf16[2048,4096]{1,0:T(8,128)(2,1)} %bitcast.80, bf16[32,8,32,128]{3,2,1,0:T(8,128)(2,1)} %bitcast.32), kind=kOutput, calls=%fused_computation.12 | convolution fusion | flops 4296015872 | bytes 19922944 | tf_op jit(solution)/shard_map/ik,jk->ij/dot_general | solution.py:329
  226.1 9.9 %all-to-all-start.2 = ((bf16[16,128,256]{2,1,0:T(8,128)(2,1)}), bf16[16,128,256]{2,1,0:T(8,128)(2,1)}, u32[]{:S(2)}, u32[]{:S(2)}) async-start(bf16[16,128,256]{2,1,0:T(8,128)(2,1)} %bitcast.87), calls=%async_computation.2 | async-start | bytes 2097152 | tf_op jit(solution)/shard_map/all_to_all | solution.py:331
  236.0 0.0 all-gather.2.cloned.1.call-start
  236.0 1.3 collective-permute-start.1
  237.3 1.5 collective-permute-start
  238.9 5.1 %broadcast_multiply_fusion.2 = (f32[256,64,64]{0,2,1:T(8,128)}, f32[256,64,64]{0,2,1:T(8,128)}, f32[256,64,64]{0,2,1:T(8,128)}) fusion(f32[256,64]{0,1:T(8,128)S(1)} %get-tuple-element.29, f32[256,64]{0,1:T(8,128)S(1)} %get-tuple-element.30, f32[256,64]{0,1:T(8,128)S(1)} %get-tuple-element.28, f32[256,64]{0,1:T(8,128)S(1)} %get-tuple-element.31), kind=kLoop, calls=%fused_computation.18 | loop fusion | flops 3145728 | bytes 12845056 | tf_op jit(solution)/shard_map/mul | solution.py:259
  243.9 15.8 %all-to-all-done.2 = bf16[16,128,256]{2,1,0:T(8,128)(2,1)} async-done(((bf16[16,128,256]{2,1,0:T(8,128)(2,1)}), bf16[16,128,256]{2,1,0:T(8,128)(2,1)}, u32[]{:S(2)}, u32[]{:S(2)}) %all-to-all-start.2) | async-done | bytes 1048608 | tf_op jit(solution)/shard_map/all_to_all | solution.py:331
  259.7 2.0 reduce_sum.85
  261.7 0.0 all-gather.2.cloned.1.call-update
  261.8 0.6 multiply_reduce_fusion.3
  262.4 0.6 multiply_reduce_fusion
  265.1 0.1 slice.54
  265.2 0.5 broadcast.309
  265.7 0.7 reduce.5
  266.4 0.1 reshape_squeeze.7
  266.4 0.6 multiply_bitcast_fusion
  267.1 1.2 copy.20
  268.3 1.6 div.56
  269.9 12.6 %fusion = f32[64,768]{1,0:T(8,128)S(1)} fusion(f32[64,4096]{1,0:T(8,128)} %div.56, f32[256,4096]{0,1:T(8,128)} %bitcast.84, f32[256,4096]{0,1:T(8,128)} %bitcast.85, f32[256,4096]{0,1:T(8,128)} %bitcast.83), kind=kOutput, calls=%fused_computation | convolution fusion | flops 2422210560 | bytes 13828096 | tf_op jit(solution)/shard_map/dot_general | solution.py:270
  282.5 0.1 fusion.37
  282.7 0.2 dynamic_update_slice.3
  282.9 41.5 %psum.7 = f32[1024]{0:T(1024)S(1)} all-reduce(f32[1024]{0:T(1024)S(1)} %pad_maximum_fusion.2), channel_id=1, replica_groups=mesh['img'=2,'band'=4,'pw'=4] {'band','pw'}, use_global_device_ids=true, to_apply=%region_5.6 | all-reduce | flops 1024 | bytes 8192 | tf_op jit(solution)/shard_map/psum | solution.py:324
  324.5 0.6 slice.55
  325.0 0.6 multiply_reduce_fusion.2
  326.3 0.6 broadcast_in_dim.24
  326.9 11.9 %fusion.6 = bf16[256,4096]{1,0:T(8,128)(2,1)S(1)} fusion(bf16[2048,256]{1,0:T(8,128)(2,1)} %all-gather.2.cloned.1.call-done, bf16[2048,4096]{1,0:T(8,128)(2,1)} %bitcast.81, bf16[32,8,32,128]{3,2,1,0:T(8,128)(2,1)} %bitcast.32), kind=kOutput, calls=%fused_computation.8 | convolution fusion | flops 4298113024 | bytes 22020096 | tf_op jit(solution)/shard_map/ij,ik->jk/dot_general | solution.py:335
  338.8 2.8 broadcast_in_dim_reshape.3
  (40 shorter events, 0.1 us)
Async XLA Ops:
  7.2 12.1 %copy-start = (bf16[1,1024,256]{2,1,0:T(8,128)(2,1)S(1)}, bf16[1,1024,256]{2,1,0:T(8,128)(2,1)}, u32[]{:S(2)}) copy-start(bf16[1,1024,256]{2,1,0:T(8,128)(2,1)} %param.16) | copy-start | bytes 1572868
  25.0 10.4 %copy-start.16 = (s32[256]{0:T(256)S(1)}, s32[256]{0:T(256)}, u32[]{:S(2)}) copy-start(s32[256]{0:T(256)} %param.20) | copy-start | bytes 3076
  25.0 10.4 %copy-start.17 = (f32[4]{0:T(128)S(1)}, f32[4]{0:T(128)}, u32[]{:S(2)}) copy-start(f32[4]{0:T(128)} %param.21) | copy-start | bytes 52
  25.0 10.5 %copy-start.13 = (s32[1,3,256]{2,0,1:T(1,128)S(1)}, s32[1,3,256]{2,0,1:T(1,128)}, u32[]{:S(2)}) copy-start(s32[1,3,256]{2,0,1:T(1,128)} %param.17) | copy-start | bytes 9220
  26.9 51.5 %all-to-all-start = ((bf16[256,32,128]{2,1,0:T(8,128)(2,1)}), bf16[256,32,128]{2,1,0:T(8,128)(2,1)S(1)}, u32[]{:S(2)}, u32[]{:S(2)}) async-start(bf16[256,32,128]{2,1,0:T(8,128)(2,1)} %bitcast.31), calls=%async_computation | async-start | bytes 4194304 | tf_op jit(solution)/shard_map/all_to_all | solution.py:304
  35.4 44.3 %copy-start.5 = (f32[512,128]{1,0:T(8,128)S(1)}, f32[512,128]{1,0:T(8,128)}, u32[]{:S(2)}) copy-start(f32[512,128]{1,0:T(8,128)} %constant.125.clone.kin_ref) | copy-start | bytes 786436
  35.4 44.3 %copy-start.6 = (bf16[2,256,256]{2,1,0:T(8,128)(2,1)S(1)}, bf16[2,256,256]{2,1,0:T(8,128)(2,1)}, u32[]{:S(2)}) copy-start(bf16[2,256,256]{2,1,0:T(8,128)(2,1)} %constant.119.clone.tz_ref) | copy-start | bytes 786436
  35.4 44.3 %copy-start.7 = (bf16[2,256,256]{2,1,0:T(8,128)(2,1)S(1)}, bf16[2,256,256]{2,1,0:T(8,128)(2,1)}, u32[]{:S(2)}) copy-start(bf16[2,256,256]{2,1,0:T(8,128)(2,1)} %constant.124.clone.bz_ref) | copy-start | bytes 786436
  35.4 44.2 %copy-start.8 = (bf16[128,64]{1,0:T(8,128)(2,1)S(1)}, bf16[128,64]{1,0:T(8,128)(2,1)}, u32[]{:S(2)}) copy-start(bf16[128,64]{1,0:T(8,128)(2,1)} %constant.120.clone.ty_ref) | copy-start | bytes 49156
  35.5 44.2 %copy-start.9 = (bf16[128,64]{1,0:T(8,128)(2,1)S(1)}, bf16[128,64]{1,0:T(8,128)(2,1)}, u32[]{:S(2)}) copy-start(bf16[128,64]{1,0:T(8,128)(2,1)} %constant.121.clone.tx_ref) | copy-start | bytes 49156
  35.5 44.2 %copy-start.10 = (bf16[64,128]{1,0:T(8,128)(2,1)S(1)}, bf16[64,128]{1,0:T(8,128)(2,1)}, u32[]{:S(2)}) copy-start(bf16[64,128]{1,0:T(8,128)(2,1)} %constant.122.clone.bx_ref) | copy-start | bytes 49156
  35.5 44.2 %copy-start.11 = (bf16[64,128]{1,0:T(8,128)(2,1)S(1)}, bf16[64,128]{1,0:T(8,128)(2,1)}, u32[]{:S(2)}) copy-start(bf16[64,128]{1,0:T(8,128)(2,1)} %constant.123.clone.by_ref) | copy-start | bytes 49156
  78.4 1.3 copy-start.12
  160.0 1.3 copy-start.3
  161.3 10.2 %copy-start.4 = (bf16[256,256]{1,0:T(8,128)(2,1)S(1)}, bf16[256,256]{1,0:T(8,128)(2,1)}, u32[]{:S(2)}) copy-start(bf16[256,256]{1,0:T(8,128)(2,1)} %constant.118.clone.r_ref) | copy-start | bytes 393220
  161.3 52.8 %all-to-all-start.1 = ((bf16[256,32,128]{2,1,0:T(8,128)(2,1)}), bf16[256,32,128]{2,1,0:T(8,128)(2,1)}, u32[]{:S(2)}, u32[]{:S(2)}) async-start(bf16[256,32,128]{2,1,0:T(8,128)(2,1)} %bitcast.79), calls=%async_computation.1 | async-start | bytes 4194304 | tf_op jit(solution)/shard_map/all_to_all | solution.py:316
  171.5 3.4 copy-start.2
  226.1 33.6 %all-to-all-start.2 = ((bf16[16,128,256]{2,1,0:T(8,128)(2,1)}), bf16[16,128,256]{2,1,0:T(8,128)(2,1)}, u32[]{:S(2)}, u32[]{:S(2)}) async-start(bf16[16,128,256]{2,1,0:T(8,128)(2,1)} %bitcast.87), calls=%async_computation.2 | async-start | bytes 2097152 | tf_op jit(solution)/shard_map/all_to_all | solution.py:331
  236.0 90.9 %all-gather.2.cloned.1.call-start = ((), (), s32[]{:S(2)}) async-start(), calls=%async_computation.3 | async-start | bytes 1114112 | tf_op jit(solution)/shard_map/all_gather | solution.py:334
  236.0 25.7 %collective-permute-start.1 = (s32[3,256]{1,0:T(4,128)S(1)}, s32[3,256]{1,0:T(4,128)S(1)}, u32[]{:S(2)}, u32[]{:S(2)}) collective-permute-start(s32[3,256]{1,0:T(4,128)S(1)} %bitcast.96), channel_id=1, source_target_pairs={{0,16},{1,17},{2,18},{3,19},{4,20},{5,21},{6,22},{7,23},{8,24},{9,... | collective-permute-start | bytes 9224 | tf_op jit(solution)/shard_map/ppermute | solution.py:28
  237.3 24.4 %collective-permute-start = (s32[3,256]{1,0:T(4,128)S(1)}, s32[3,256]{1,0:T(4,128)S(1)}, u32[]{:S(2)}, u32[]{:S(2)}) collective-permute-start(s32[3,256]{1,0:T(4,128)S(1)} %bitcast.97), channel_id=1, source_target_pairs={{16,0},{17,1},{18,2},{19,3},{20,4},{21,5},{22,6},{23,7},{24,8},{25... | collective-permute-start | bytes 9224 | tf_op jit(solution)/shard_map/ppermute | solution.py:28
  238.9 22.9 %copy-start.14 = (s32[3,256]{1,0:T(4,128)S(1)}, s32[3,256]{1,0:T(4,128)}, u32[]{:S(2)}) copy-start(s32[3,256]{1,0:T(4,128)} %param.18) | copy-start | bytes 9220
  238.9 22.9 %copy-start.15 = (s32[3,256]{1,0:T(4,128)S(1)}, s32[3,256]{1,0:T(4,128)}, u32[]{:S(2)}) copy-start(s32[3,256]{1,0:T(4,128)} %param.19) | copy-start | bytes 9220
  326.9 14.7 %copy-start.1 = (bf16[1,1024,256]{2,1,0:T(8,128)(2,1)S(1)}, bf16[1,1024,256]{2,1,0:T(8,128)(2,1)}, u32[]{:S(2)}) copy-start(bf16[1,1024,256]{2,1,0:T(8,128)(2,1)} %param.16) | copy-start | bytes 1572868
Sparse Core Ops, SparseCore 0:
  261.9 55.5 all-gather.1
where the time goes:
time: 356 us; the launch traced here: 349 us
  Pallas kernels  86.9 us (24%)
  waiting for transfers between devices  82.9 us (23%)
  matrix products  48.5 us (14%)
  blocking collectives  41.5 us (12%)
  starting transfers between devices  31.4 us (9%)
  local copies, waits for them, and re-layouts  27.7 us (8%)
  between operations  17.5 us (5%)
  other arithmetic  12.4 us (3%)
    pallas_call x1, Pallas kernels, apply_local(): pl.pallas_call(apply_kernel, grid=(vectors // 2,), in_specs=[pl.BlockSpec...  80.3 us
    psum x1, blocking collectives, body(): lax.psum(jnp.concatenate([force_part.reshape(-1), ritz_part]), axes)  41.5 us
    all_to_all x1, waiting for transfers between devices, body(): lax.all_to_all(orbitals, axes, split_axis=0, concat_axis=0, tiled=True)  34.6 us
    all_to_all x1, waiting for transfers between devices, body(): lax.all_to_all(search, axes, split_axis=0, concat_axis=0, tiled=True)  32.5 us
    unnamed x39, local copies, waits for them, and re-layouts  20 us
    all_to_all x1, waiting for transfers between devices, body(): lax.all_to_all(partial, axes, split_axis=0, concat_axis=0, tiled=True)  15.8 us
    dot_general x1, matrix products, atom_forces(): moments = jnp.dot(density, stacked.T, precision=highest)  12.6 us
    dot_general x1, matrix products, body(): jnp.einsum('ik,jk->ij', stacked, search, preferred_element_type=jnp.float32)  12.1 us
  transfers between devices with their start and end apart: 6, of which 3 were waited for; matrix products, arithmetic and copies ran while one was open for 10% of the time, Pallas kernels for 2%

commit v1 on v0

--- a/solution.py
+++ b/solution.py
@@ -78,126 +78,195 @@
     return jnp.dot(left, right, preferred_element_type=jnp.float32)
 
 
+MESH_ID = pl.DeviceIdType.MESH
+GROUP = ("band", "pw")
+
+
+def group_place():
+    inner = lax.axis_size(GROUP[1])
+    count = lax.axis_size(GROUP[0]) * inner
+    mine = lax.axis_index(GROUP[0]) * inner + lax.axis_index(GROUP[1])
+    return mine, count, inner
+
+
+def device_of(index, inner):
+    return {GROUP[0]: index // inner, GROUP[1]: lax.rem(index, inner)}
+
+
+def greet_all(mine, count, inner):
+    barrier = pltpu.get_barrier_semaphore()
+    for k in range(1, count):
+        peer = lax.rem(mine + k, count)
+        pl.semaphore_signal(
+            barrier, inc=1, device_id=device_of(peer, inner), device_id_type=MESH_ID
+        )
+    pl.semaphore_wait(barrier, count - 1)
+
+
 def apply_kernel(
-    vec_ref, pot_ref, kin_ref, tz_ref, ty_ref, tx_ref, bx_ref, by_ref, bz_ref,
-    out_ref, ritz_ref, dens_ref, zs_ref, s_ref,
+    orb_ref, pot_ref, kin_ref, tz_ref, ty_ref, tx_ref, bx_ref, by_ref, bz_ref,
+    out_ref, ritz_ref, dens_ref,
+    in_ref, back_ref, zs_ref, s_ref, send_sem, recv_sem, back_send_sem, back_recv_sem,
 ):
     lanes = 2 * G
     half = W // 2
     rows = W * half
     bf = jnp.bfloat16
-
-    @pl.when(pl.program_id(0) == 0)
-    def _():
-        dens_ref[...] = jnp.zeros_like(dens_ref)
-
-    def pair_in():
-        return jnp.concatenate(
-            [vec_ref[:, v].reshape(rows, 4 * W) for v in range(2)], axis=1
+    mine, count, inner = group_place()
+    chunks = orb_ref.shape[1] // 2
+
+    greet_all(mine, count, inner)
+
+    def send_chunk(c, carry):
+        at = pl.ds(2 * c, 2)
+        for k in range(1, count):
+            peer = lax.rem(mine + k, count)
+            pltpu.make_async_remote_copy(
+                src_ref=orb_ref.at[peer, at],
+                dst_ref=in_ref.at[mine, at],
+                send_sem=send_sem.at[c],
+                recv_sem=recv_sem.at[c],
+                device_id=device_of(peer, inner),
+                device_id_type=MESH_ID,
+            ).start()
+        return carry
+
+    lax.fori_loop(0, chunks, send_chunk, 0)
+    in_ref[mine] = orb_ref[mine]
+    dens_ref[...] = jnp.zeros_like(dens_ref)
+
+    def all_of(ref, c, sem):
+        part = ref.at[pl.ds(0, count - 1), pl.ds(2 * c, 2)]
+        return pltpu.make_async_copy(part, part, sem.at[c])
+
+    def chunk_step(c, chunk_carry):
+        all_of(in_ref, c, recv_sem).wait()
+        vecs = jnp.concatenate(
+            [in_ref[:, 2 * c + v].reshape(rows, 4 * W) for v in range(2)], axis=1
         )
-
-    vecs = pair_in()
-    for p in range(2):
-        zs_ref[p] = mm(vecs, tz_ref[p]).astype(bf)
-
-    def y_step(i, carry):
-        cols = []
-        for k in range(2):
-            at = pl.ds(pl.multiple_of((2 * i + k) * half, half), half)
-            parts = [zs_ref[p, at, d * lanes : (d + 1) * lanes] for p in range(2) for d in range(2)]
-            cols.append(jnp.concatenate(parts, axis=0))
-        done = mm(ty_ref[...], jnp.concatenate(cols, axis=1))
-        for k in range(2):
-            at = pl.ds(pl.multiple_of((2 * i + k) * lanes, lanes), lanes)
-            s_ref[at, :] = done[:, k * lanes : (k + 1) * lanes]
+        for p in range(2):
+            zs_ref[p] = mm(vecs, tz_ref[p]).astype(bf)
+
+        def y_step(i, carry):
+            cols = []
+            for k in range(2):
+                at = pl.ds(pl.multiple_of((2 * i + k) * half, half), half)
+                parts = [
+                    zs_ref[p, at, d * lanes : (d + 1) * lanes] for p in range(2) for d in range(2)
+                ]
+                cols.append(jnp.concatenate(parts, axis=0))
+            done = mm(ty_ref[...], jnp.concatenate(cols, axis=1))
+            for k in range(2):
+                at = pl.ds(pl.multiple_of((2 * i + k) * lanes, lanes), lanes)
+                s_ref[at, :] = done[:, k * lanes : (k + 1) * lanes]
+            return carry
+
+        lax.fori_loop(0, W // 2, y_step, 0, unroll=4)
+
+        def x_step(i, carry):
+            ats = [pl.ds(2 * i + k, 2 * W, stride=G) for k in range(2)]
+            cols = [s_ref[at, :].astype(bf) for at in ats]
+            done = mm(tx_ref[...], jnp.concatenate(cols, axis=1))
+            real, imag = (done[:G], done[G:])
+            pot = jnp.concatenate([pot_ref[2 * i], pot_ref[2 * i + 1]], axis=1)
+            square = real * real + imag * imag
+            for k in range(2):
+                dens_ref[2 * i + k] += square[:, k * lanes : (k + 1) * lanes]
+            weighted = jnp.concatenate([(real * pot).astype(bf), (imag * pot).astype(bf)], axis=0)
+            back = mm(bx_ref[...], weighted)
+            for k in range(2):
+                s_ref[ats[k], :] = back[:, k * lanes : (k + 1) * lanes]
+            return carry
+
+        lax.fori_loop(0, G // 2, x_step, 0, unroll=4)
+
+        def back_y_step(i, carry):
+            cols = []
+            for k in range(2):
+                at = pl.ds(pl.multiple_of((2 * i + k) * lanes, lanes), lanes)
+                cols.append(s_ref[at, :].astype(bf))
+            done = mm(by_ref[...], jnp.concatenate(cols, axis=1)).astype(bf)
+            for k in range(2):
+                at = pl.ds(pl.multiple_of((2 * i + k) * half, half), half)
+                for p in range(2):
+                    for q in range(2):
+                        r = (2 * p + q) * half
+                        zs_ref[p, at, q * lanes : (q + 1) * lanes] = done[
+                            r : r + half, k * lanes : (k + 1) * lanes
+                        ]
+            return carry
+
+        lax.fori_loop(0, W // 2, back_y_step, 0, unroll=4)
+
+        local = mm(zs_ref[0], bz_ref[0]) + mm(zs_ref[1], bz_ref[1])
+        kin = kin_ref[...]
+        npw_total = W * W * W
+        for v in range(2):
+            orb = in_ref[:, 2 * c + v].reshape(rows, 4 * W).astype(jnp.float32)
+            ham = kin * orb + local[:, v * 4 * W : (v + 1) * 4 * W]
+            numerator = jnp.sum(jnp.sum(orb * ham, axis=0, keepdims=True), axis=1, keepdims=True)
+            denominator = jnp.sum(jnp.sum(orb * orb, axis=0, keepdims=True), axis=1, keepdims=True)
+            ritz = numerator / npw_total / (denominator / npw_total + epsilon)
+            search = ((ham - ritz * orb) / (1.0 + kin)).astype(bf)
+            back_ref[:, 2 * c + v] = search.reshape(in_ref.shape[0], *in_ref.shape[2:])
+            ritz_ref[c, :, v * 128 : (v + 1) * 128] = jnp.broadcast_to(ritz, (8, 128))
+        at = pl.ds(2 * c, 2)
+        out_ref[mine, at] = back_ref[mine, at]
+        for k in range(1, count):
+            peer = lax.rem(mine + k, count)
+            pltpu.make_async_remote_copy(
+                src_ref=back_ref.at[peer, at],
+                dst_ref=out_ref.at[mine, at],
+                send_sem=back_send_sem.at[c],
+                recv_sem=back_recv_sem.at[c],
+                device_id=device_of(peer, inner),
+                device_id_type=MESH_ID,
+            ).start()
+        return chunk_carry
+
+    lax.fori_loop(0, chunks, chunk_step, 0)
+
+    def finish(c, carry):
+        all_of(in_ref, c, send_sem).wait()
+        all_of(out_ref, c, back_send_sem).wait()
+        all_of(out_ref, c, back_recv_sem).wait()
         return carry
 
-    lax.fori_loop(0, W // 2, y_step, 0, unroll=4)
-
-    def x_step(i, carry):
-        ats = [pl.ds(2 * i + k, 2 * W, stride=G) for k in range(2)]
-        cols = [s_ref[at, :].astype(bf) for at in ats]
-        done = mm(tx_ref[...], jnp.concatenate(cols, axis=1))
-        real, imag = (done[:G], done[G:])
-        pot = jnp.concatenate([pot_ref[2 * i], pot_ref[2 * i + 1]], axis=1)
-        square = real * real + imag * imag
-        for k in range(2):
-            dens_ref[2 * i + k] += square[:, k * lanes : (k + 1) * lanes]
-        weighted = jnp.concatenate([(real * pot).astype(bf), (imag * pot).astype(bf)], axis=0)
-        back = mm(bx_ref[...], weighted)
-        for k in range(2):
-            s_ref[ats[k], :] = back[:, k * lanes : (k + 1) * lanes]
-        return carry
-
-    lax.fori_loop(0, G // 2, x_step, 0, unroll=4)
-
-    def back_y_step(i, carry):
-        cols = []
-        for k in range(2):
-            at = pl.ds(pl.multiple_of((2 * i + k) * lanes, lanes), lanes)
-            cols.append(s_ref[at, :].astype(bf))
-        done = mm(by_ref[...], jnp.concatenate(cols, axis=1)).astype(bf)
-        for k in range(2):
-            at = pl.ds(pl.multiple_of((2 * i + k) * half, half), half)
-            for p in range(2):
-                for c in range(2):
-                    r = (2 * p + c) * half
-                    zs_ref[p, at, c * lanes : (c + 1) * lanes] = done[
-                        r : r + half, k * lanes : (k + 1) * lanes
-                    ]
-        return carry
-
-    lax.fori_loop(0, W // 2, back_y_step, 0, unroll=4)
-
-    local = mm(zs_ref[0], bz_ref[0]) + mm(zs_ref[1], bz_ref[1])
-    kin = kin_ref[...]
-    npw_total = W * W * W
-    for v in range(2):
-        orb = vec_ref[:, v].reshape(rows, 4 * W).astype(jnp.float32)
-        ham = kin * orb + local[:, v * 4 * W : (v + 1) * 4 * W]
-        numerator = jnp.sum(jnp.sum(orb * ham, axis=0, keepdims=True), axis=1, keepdims=True)
-        denominator = jnp.sum(jnp.sum(orb * orb, axis=0, keepdims=True), axis=1, keepdims=True)
-        ritz = numerator / npw_total / (denominator / npw_total + epsilon)
-        search = ((ham - ritz * orb) / (1.0 + kin)).astype(bf)
-        out_ref[:, v] = search.reshape(vec_ref.shape[0], *vec_ref.shape[2:])
-        ritz_ref[0, :, v * 128 : (v + 1) * 128] = jnp.broadcast_to(ritz, (8, 128))
-
-
-def apply_local(whole, potential):
-    devices, vectors, planes, half, lanes = whole.shape
+    lax.fori_loop(0, chunks, finish, 0)
+
+
+def apply_all(orbitals, potential):
+    devices, vectors, planes, half, lanes = orbitals.shape
     tabs = kernel_tables()
     kin = jnp.asarray(kinetic_table())
-    block = (devices, 2, planes, half, lanes)
-
-    def fixed(arr):
-        return pl.BlockSpec(arr.shape, lambda p, n=arr.ndim: (0,) * n)
-
+    whole = pl.BlockSpec(memory_space=pltpu.VMEM)
+    chunks = vectors // 2
     flops = vectors * 2 * 2 * (W * W * 2 * W * 2 * G + W * G * 2 * W * 2 * G + G * G * 2 * W * 2 * G)
     return pl.pallas_call(
         apply_kernel,
-        grid=(vectors // 2,),
-        in_specs=[pl.BlockSpec(block, lambda p: (0, p, 0, 0, 0)), fixed(potential), fixed(kin)]
-        + [fixed(t) for t in tabs],
-        out_specs=[
-            pl.BlockSpec(block, lambda p: (0, p, 0, 0, 0)),
-            pl.BlockSpec((1, 8, 256), lambda p: (p, 0, 0)),
-            pl.BlockSpec((G, G, 2 * G), lambda p: (0, 0, 0)),
-        ],
+        in_specs=[whole] * 9,
+        out_specs=[whole] * 3,
         out_shape=[
-            jax.ShapeDtypeStruct(whole.shape, jnp.bfloat16),
-            jax.ShapeDtypeStruct((vectors // 2, 8, 256), jnp.float32),
+            jax.ShapeDtypeStruct(orbitals.shape, jnp.bfloat16),
+            jax.ShapeDtypeStruct((chunks, 8, 256), jnp.float32),
             jax.ShapeDtypeStruct((G, G, 2 * G), jnp.float32),
         ],
         scratch_shapes=[
+            pltpu.VMEM(orbitals.shape, jnp.bfloat16),
+            pltpu.VMEM(orbitals.shape, jnp.bfloat16),
             pltpu.VMEM((2, W * W // 2, 4 * G), jnp.bfloat16),
             pltpu.VMEM((W * 2 * G, 2 * G), jnp.float32),
+            pltpu.SemaphoreType.DMA((chunks,)),
+            pltpu.SemaphoreType.DMA((chunks,)),
+            pltpu.SemaphoreType.DMA((chunks,)),
+            pltpu.SemaphoreType.DMA((chunks,)),
         ],
         compiler_params=pltpu.CompilerParams(
-            dimension_semantics=("arbitrary",), vmem_limit_bytes=48 * 1024 * 1024
+            collective_id=0, has_side_effects=True, vmem_limit_bytes=44 * 1024 * 1024
         ),
         cost_estimate=pl.CostEstimate(flops=flops, bytes_accessed=8 << 20, transcendentals=0),
-        name="apply_local",
-    )(whole, potential, kin, *tabs)
+        name="apply_all",
+    )(orbitals, potential, kin, *tabs)
 
 
 def turn_kernel(c_ref, r_ref, out_ref):
@@ -301,8 +370,7 @@
     vectors = BLOCK // devices
     orbitals = jnp.einsum("ib,ik->bk", rotation[0], flat_all, preferred_element_type=jnp.float32)
     orbitals = orbitals.astype(jnp.bfloat16).reshape(BLOCK, planes * (W // 2), 4 * W)
-    whole = lax.all_to_all(orbitals, axes, split_axis=0, concat_axis=0, tiled=True)
-    whole = whole.reshape(devices, vectors, planes, W // 2, 4 * W)
+    orbitals = orbitals.reshape(devices, vectors, planes, W // 2, 4 * W)
     both = with_turned(flat_all)
     kind_ids = jnp.arange(SPECIES, dtype=jnp.int32)
     strength = jnp.sum(jnp.where(species[:, None] == kind_ids[None, :], depth[None, :], 0.0), 1)
@@ -311,9 +379,7 @@
     potential, joined = local_potential(tables, strength)
     potential = jnp.swapaxes(potential.reshape(G, G, G), 0, 1)
     potential = jnp.concatenate([potential, potential], 2)
-    search, ritz, density = apply_local(whole, potential)
-    search = search.reshape(BLOCK, planes * (W // 2), 4 * W)
-    search = lax.all_to_all(search, axes, split_axis=0, concat_axis=0, tiled=True)
+    search, ritz, density = apply_all(orbitals, potential)
     search = search.reshape(BLOCK, -1)
     density = jnp.swapaxes(density[:, :, :G] + density[:, :, G:], 0, 1).reshape(G, G * G) / BLOCK
     force_part = atom_forces(density, tables, joined, strength)

time: 356 us -> 288 us (0.81)
  waiting for transfers between devices: 82.9 us -> 16 us
  starting transfers between devices: 31.4 us -> 7.39 us
  Pallas kernels: 86.9 us -> 109 us
  local copies, waits for them, and re-layouts: 27.7 us -> 32.9 us
    all_to_all x2 -> x0, waiting for transfers between devices: 67.1 us -> none  [the longest x1 34.6 us: body(): lax.all_to_all(orbitals, axes, split_axis=0, concat_axis=0, tiled=True)]
    pallas_call x1, Pallas kernels: 80.3 us -> 102 us  [apply_all(): pl.pallas_call(apply_kernel, in_specs=[whole] * 9, out_specs=[whole] * 3,...]
    all_to_all x2 -> x0, starting transfers between devices: 18.7 us -> none  [the longest x1 10.2 us: body(): lax.all_to_all(search, axes, split_axis=0, concat_axis=0, tiled=True)]
    all_to_all x1, starting transfers between devices: 9.85 us -> 4.76 us  [body(): lax.all_to_all(partial, axes, split_axis=0, concat_axis=0, tiled=True)]
    reshape x0 -> x1, local copies, waits for them, and re-layouts: none -> 4.38 us  [body(): search = search.reshape(BLOCK, -1)]
  transfers between devices with their start and end apart: 6 -> 4, of which waited for: 3 -> 1; matrix products, arithmetic and copies ran while one was open for 10% -> 11% of each run, Pallas kernels for 2% -> 0%
where the time goes in v1:
time: 288 us; the launch traced here: 283 us
  Pallas kernels  109 us (38%)
  matrix products  45.5 us (16%)
  blocking collectives  41.6 us (14%)
  local copies, waits for them, and re-layouts  32.9 us (11%)
  between operations  17.5 us (6%)
  waiting for transfers between devices  16 us (6%)
  other arithmetic  12.5 us (4%)
  starting transfers between devices  7.39 us (3%)
    pallas_call x1, Pallas kernels, apply_all(): pl.pallas_call(apply_kernel, in_specs=[whole] * 9, out_specs=[whole] * 3,...  102 us
    psum x1, blocking collectives, body(): lax.psum(jnp.concatenate([force_part.reshape(-1), ritz_part]), axes)  41.6 us
    unnamed x39, local copies, waits for them, and re-layouts  17.5 us
    all_to_all x1, waiting for transfers between devices, body(): lax.all_to_all(partial, axes, split_axis=0, concat_axis=0, tiled=True)  16 us
    dot_general x1, matrix products, atom_forces(): moments = jnp.dot(density, stacked.T, precision=highest)  12.8 us
    dot_general x1, matrix products, body(): jnp.einsum('ij,ik->jk', intersections, stacked, preferred_element_type=jn...  12.1 us
    dot_general x1, matrix products, body(): jnp.einsum('ik,jk->ij', stacked, search, preferred_element_type=jnp.float32)  12 us
    pallas_call x1, Pallas kernels, with_turned(): pl.pallas_call(turn_kernel, grid=(bands // tile,), in_specs=[pl.BlockSpec...  6.88 us
  transfers between devices with their start and end apart: 4, of which 1 were waited for; matrix products, arithmetic and copies ran while one was open for 11% of the time, Pallas kernels for 0%

profile of v1, /device:TPU:0, one launch (start us, length us, event | category | flops | bytes accessed | tf_op | source)
XLA Modules:
  0.0 282.6 jit_solution(4773245181579496394)
XLA Ops:
  7.2 0.0 copy-start
  7.2 0.0 copy-start.4
  7.2 12.1 %copy.22 = bf16[128,8,2,2048]{3,1,2,0:T(8,128)(2,1)} copy(bf16[128,8,2,2048]{3,2,1,0:T(2,128)(2,1)} %bitcast.79) | data formatting | bytes 16777216
  19.3 3.4 %copy-done.2 = bf16[128,8,2,2048]{3,1,2,0:T(8,128)(2,1)S(1)} copy-done((bf16[128,8,2,2048]{3,1,2,0:T(8,128)(2,1)S(1)}, bf16[128,8,2,2048]{3,1,2,0:T(8,128)(2,1)}, u32[]{:S(2)}) %copy-start.2) | copy-done | bytes 8388632
  22.7 6.9 %with_turned.1 = bf16[2,1024,4096]{2,1,0:T(8,128)(2,1)} custom-call(bf16[1024,4096]{1,0:T(8,128)(2,1)S(1)} %bitcast.74, bf16[256,256]{1,0:T(8,128)(2,1)S(1)} %copy-done.4), custom_call_target="tpu_custom_call" | custom-call | flops 2147483648 | bytes 25165824 | tf_op jit(solution)/shard_map/with_turned/pallas_call | solution.py:289
  29.6 2.4 fusion.13
  32.0 0.0 copy-start.13
  32.0 0.0 copy-start.16
  32.0 0.5 copy.23
  32.5 0.2 copy-done.13
  32.7 0.0 copy-start.9
  32.7 0.0 copy-start.10
  32.7 0.0 copy-start.11
  32.7 0.1 fusion.39
  32.8 0.1 select_reduce_fusion
  32.9 6.1 %fusion.10 = f32[64,64,64]{2,1,0:T(8,128)S(1)} fusion(f32[256,64]{0,1:T(8,128)S(1)} %get-tuple-element.29, f32[256,64]{0,1:T(8,128)S(1)} %get-tuple-element.30, s32[256]{0:T(256)S(1)} %bitcast.85, f32[256]{0:T(256)S(1)} %select_reduce_fusion), kind=kOutput, calls=%fused_computation.18 | convolution fusion | flops 806666240 | bytes 1181696 | tf_op jit(solution)/shard_map/dot_general | solution.py:329
  39.1 0.6 pad_maximum_fusion.pot_ref
  39.8 102.3 %apply_all.1 = (bf16[16,16,2,16,128]{4,3,2,1,0:T(8,128)(2,1)S(1)}, f32[8,8,256]{2,1,0:T(8,128)S(1)}, f32[64,64,128]{2,1,0:T(8,128)S(1)}) custom-call(bf16[16,16,2,16,128]{4,3,2,1,0:T(8,128)(2,1)S(1)} %bitcast.76, f32[64,64,128]{2,1,0:T(8,128)S(1)} %pad_maximum_fusion.pot_ref, f32[512,128]{1,0:T(8,128)S(1)} %copy-done.5, bf16[2,256,256]{2,1,0:T(8,128)(2,1)S(1)} %copy-done.6, ...), custom_call_target="tpu_custom_call" | custom-call | flops 3758096384 | bytes 8388608 | tf_op jit(solution)/shard_map/apply_all/pallas_call | solution.py:245
  142.1 0.0 copy-start.3
  142.1 1.3 copy-done.3
  143.4 4.4 %reshape.222 = bf16[256,4096]{1,0:T(8,128)(2,1)} reshape(bf16[16,16,2,16,128]{4,3,2,1,0:T(8,128)(2,1)} %copy-done.3) | data formatting | bytes 4194304 | tf_op jit(solution)/shard_map/reshape | solution.py:383
  147.8 12.0 %fusion.9 = bf16[2048,256]{1,0:T(8,128)(2,1)} fusion(bf16[2048,4096]{1,0:T(8,128)(2,1)} %bitcast.77, bf16[256,4096]{1,0:T(8,128)(2,1)} %reshape.222), kind=kOutput, calls=%fused_computation.12 | convolution fusion | flops 4296015872 | bytes 19922944 | tf_op jit(solution)/shard_map/ik,jk->ij/dot_general | solution.py:395
  159.8 4.8 %all-to-all-start = ((bf16[16,128,256]{2,1,0:T(8,128)(2,1)}), bf16[16,128,256]{2,1,0:T(8,128)(2,1)}, u32[]{:S(2)}, u32[]{:S(2)}) async-start(bf16[16,128,256]{2,1,0:T(8,128)(2,1)} %bitcast.83), calls=%async_computation | async-start | bytes 2097152 | tf_op jit(solution)/shard_map/all_to_all | solution.py:397
  164.6 0.0 all-gather.2.cloned.1.call-start
  164.7 1.3 collective-permute-start.1
  166.0 1.3 collective-permute-start
  167.3 5.1 %broadcast_multiply_fusion.2 = (f32[256,64,64]{0,2,1:T(8,128)}, f32[256,64,64]{0,2,1:T(8,128)}, f32[256,64,64]{0,2,1:T(8,128)}) fusion(f32[256,64]{0,1:T(8,128)S(1)} %get-tuple-element.29, f32[256,64]{0,1:T(8,128)S(1)} %get-tuple-element.30, f32[256,64]{0,1:T(8,128)S(1)} %get-tuple-element.28, f32[256,64]{0,1:T(8,128)S(1)} %get-tuple-element.31), kind=kLoop, calls=%fused_computation.17 | loop fusion | flops 3145728 | bytes 12845056 | tf_op jit(solution)/shard_map/mul | solution.py:328
  172.4 16.0 %all-to-all-done = bf16[16,128,256]{2,1,0:T(8,128)(2,1)} async-done(((bf16[16,128,256]{2,1,0:T(8,128)(2,1)}), bf16[16,128,256]{2,1,0:T(8,128)(2,1)}, u32[]{:S(2)}, u32[]{:S(2)}) %all-to-all-start) | async-done | bytes 1048608 | tf_op jit(solution)/shard_map/all_to_all | solution.py:397
  188.4 2.0 reduce_sum.85
  190.4 0.0 all-gather.2.cloned.1.call-update
  190.4 1.9 multiply_bitcast_fusion
  192.4 0.1 slice.54
  192.4 0.5 broadcast.309
  193.0 0.7 reduce.5
  193.6 0.1 reshape_squeeze.7
  193.7 2.8 copy.20
  196.5 1.6 div.56
  198.1 12.8 %fusion = f32[64,768]{1,0:T(8,128)S(1)} fusion(f32[64,4096]{1,0:T(8,128)} %div.56, f32[256,4096]{0,1:T(8,128)} %bitcast.81, f32[256,4096]{0,1:T(8,128)} %bitcast.82, f32[256,4096]{0,1:T(8,128)} %bitcast.80), kind=kOutput, calls=%fused_computation | convolution fusion | flops 2422210560 | bytes 13828096 | tf_op jit(solution)/shard_map/dot_general | solution.py:339
  210.9 0.1 fusion.35
  211.1 0.2 dynamic_update_slice.3
  211.3 41.6 %psum.7 = f32[1024]{0:T(1024)S(1)} all-reduce(f32[1024]{0:T(1024)S(1)} %pad_maximum_fusion.2), channel_id=1, replica_groups=mesh['img'=2,'band'=4,'pw'=4] {'band','pw'}, use_global_device_ids=true, to_apply=%region_5.6 | all-reduce | flops 1024 | bytes 8192 | tf_op jit(solution)/shard_map/psum | solution.py:390
  252.9 0.6 slice.55
  253.5 0.6 multiply_reduce_fusion.3
  254.1 0.6 multiply_reduce_fusion
  256.8 0.6 multiply_reduce_fusion.2
  258.1 0.6 broadcast_in_dim.24
  258.7 12.1 %fusion.6 = bf16[256,4096]{1,0:T(8,128)(2,1)} fusion(bf16[2048,256]{1,0:T(8,128)(2,1)} %all-gather.2.cloned.1.call-done, bf16[2048,4096]{1,0:T(8,128)(2,1)} %bitcast.78, bf16[256,4096]{1,0:T(8,128)(2,1)S(1)} %copy-done.12), kind=kOutput, calls=%fused_computation.8 | convolution fusion | flops 4298113024 | bytes 22020096 | tf_op jit(solution)/shard_map/ij,ik->jk/dot_general | solution.py:401
  270.8 4.5 %broadcast_in_dim_reshape.3 = bf16[1,256,2,2048]{3,2,1,0:T(2,128)(2,1)} reshape(bf16[256,4096]{1,0:T(8,128)(2,1)} %fusion.6) | data formatting | bytes 4194304 | tf_op jit(solution)/shard_map/broadcast_in_dim;reshape | solution.py:412
  (37 shorter events, 0.1 us)
Async XLA Ops:
  7.2 22.4 %copy-start = (bf16[1,1024,256]{2,1,0:T(8,128)(2,1)S(1)}, bf16[1,1024,256]{2,1,0:T(8,128)(2,1)}, u32[]{:S(2)}) copy-start(bf16[1,1024,256]{2,1,0:T(8,128)(2,1)} %param.16) | copy-start | bytes 1572868
  7.2 12.1 %copy-start.4 = (bf16[256,256]{1,0:T(8,128)(2,1)S(1)}, bf16[256,256]{1,0:T(8,128)(2,1)}, u32[]{:S(2)}) copy-start(bf16[256,256]{1,0:T(8,128)(2,1)} %constant.118.clone.r_ref) | copy-start | bytes 393220
  19.3 3.4 %copy-start.2 = (bf16[128,8,2,2048]{3,1,2,0:T(8,128)(2,1)S(1)}, bf16[128,8,2,2048]{3,1,2,0:T(8,128)(2,1)}, u32[]{:S(2)}) copy-start(bf16[128,8,2,2048]{3,1,2,0:T(8,128)(2,1)} %copy.22) | copy-start | bytes 25165828
  32.0 0.7 copy-start.13
  32.0 0.8 copy-start.16
  32.0 0.8 copy-start.17
  32.6 7.0 %copy-start.5 = (f32[512,128]{1,0:T(8,128)S(1)}, f32[512,128]{1,0:T(8,128)}, u32[]{:S(2)}) copy-start(f32[512,128]{1,0:T(8,128)} %constant.125.clone.kin_ref) | copy-start | bytes 786436
  32.6 7.0 %copy-start.6 = (bf16[2,256,256]{2,1,0:T(8,128)(2,1)S(1)}, bf16[2,256,256]{2,1,0:T(8,128)(2,1)}, u32[]{:S(2)}) copy-start(bf16[2,256,256]{2,1,0:T(8,128)(2,1)} %constant.119.clone.tz_ref) | copy-start | bytes 786436
  32.6 7.1 %copy-start.7 = (bf16[2,256,256]{2,1,0:T(8,128)(2,1)S(1)}, bf16[2,256,256]{2,1,0:T(8,128)(2,1)}, u32[]{:S(2)}) copy-start(bf16[2,256,256]{2,1,0:T(8,128)(2,1)} %constant.124.clone.bz_ref) | copy-start | bytes 786436
  32.6 7.1 %copy-start.8 = (bf16[128,64]{1,0:T(8,128)(2,1)S(1)}, bf16[128,64]{1,0:T(8,128)(2,1)}, u32[]{:S(2)}) copy-start(bf16[128,64]{1,0:T(8,128)(2,1)} %constant.120.clone.ty_ref) | copy-start | bytes 49156
  32.7 7.1 %copy-start.9 = (bf16[128,64]{1,0:T(8,128)(2,1)S(1)}, bf16[128,64]{1,0:T(8,128)(2,1)}, u32[]{:S(2)}) copy-start(bf16[128,64]{1,0:T(8,128)(2,1)} %constant.121.clone.tx_ref) | copy-start | bytes 49156
  32.7 7.1 %copy-start.10 = (bf16[64,128]{1,0:T(8,128)(2,1)S(1)}, bf16[64,128]{1,0:T(8,128)(2,1)}, u32[]{:S(2)}) copy-start(bf16[64,128]{1,0:T(8,128)(2,1)} %constant.122.clone.bx_ref) | copy-start | bytes 49156
  32.7 7.1 %copy-start.11 = (bf16[64,128]{1,0:T(8,128)(2,1)S(1)}, bf16[64,128]{1,0:T(8,128)(2,1)}, u32[]{:S(2)}) copy-start(bf16[64,128]{1,0:T(8,128)(2,1)} %constant.123.clone.by_ref) | copy-start | bytes 49156
  142.1 1.3 copy-start.3
  159.8 28.5 %all-to-all-start = ((bf16[16,128,256]{2,1,0:T(8,128)(2,1)}), bf16[16,128,256]{2,1,0:T(8,128)(2,1)}, u32[]{:S(2)}, u32[]{:S(2)}) async-start(bf16[16,128,256]{2,1,0:T(8,128)(2,1)} %bitcast.83), calls=%async_computation | async-start | bytes 2097152 | tf_op jit(solution)/shard_map/all_to_all | solution.py:397
  164.6 94.1 %all-gather.2.cloned.1.call-start = ((), (), s32[]{:S(2)}) async-start(), calls=%async_computation.1 | async-start | bytes 1114112 | tf_op jit(solution)/shard_map/all_gather | solution.py:400
  164.7 88.8 %collective-permute-start.1 = (s32[3,256]{1,0:T(4,128)S(1)}, s32[3,256]{1,0:T(4,128)S(1)}, u32[]{:S(2)}, u32[]{:S(2)}) collective-permute-start(s32[3,256]{1,0:T(4,128)S(1)} %bitcast.92), channel_id=1, source_target_pairs={{0,16},{1,17},{2,18},{3,19},{4,20},{5,21},{6,22},{7,23},{8,24},{9,... | collective-permute-start | bytes 9224 | tf_op jit(solution)/shard_map/ppermute | solution.py:28
  166.0 87.5 %collective-permute-start = (s32[3,256]{1,0:T(4,128)S(1)}, s32[3,256]{1,0:T(4,128)S(1)}, u32[]{:S(2)}, u32[]{:S(2)}) collective-permute-start(s32[3,256]{1,0:T(4,128)S(1)} %bitcast.93), channel_id=1, source_target_pairs={{16,0},{17,1},{18,2},{19,3},{20,4},{21,5},{22,6},{23,7},{24,8},{25... | collective-permute-start | bytes 9224 | tf_op jit(solution)/shard_map/ppermute | solution.py:28
  198.1 55.4 %copy-start.14 = (s32[3,256]{1,0:T(4,128)S(1)}, s32[3,256]{1,0:T(4,128)}, u32[]{:S(2)}) copy-start(s32[3,256]{1,0:T(4,128)} %param.18) | copy-start | bytes 9220
  198.1 55.4 %copy-start.15 = (s32[3,256]{1,0:T(4,128)S(1)}, s32[3,256]{1,0:T(4,128)}, u32[]{:S(2)}) copy-start(s32[3,256]{1,0:T(4,128)} %param.19) | copy-start | bytes 9220
  198.1 60.5 %copy-start.12 = (bf16[256,4096]{1,0:T(8,128)(2,1)S(1)}, bf16[256,4096]{1,0:T(8,128)(2,1)}, u32[]{:S(2)}) copy-start(bf16[256,4096]{1,0:T(8,128)(2,1)} %reshape.222) | copy-start | bytes 6291460
  258.7 16.6 %copy-start.1 = (bf16[1,1024,256]{2,1,0:T(8,128)(2,1)S(1)}, bf16[1,1024,256]{2,1,0:T(8,128)(2,1)}, u32[]{:S(2)}) copy-start(bf16[1,1024,256]{2,1,0:T(8,128)(2,1)} %param.16) | copy-start | bytes 1572868
Sparse Core Ops, SparseCore 0:
  190.5 55.5 all-gather.1

commit v2 on v1

--- a/solution.py
+++ b/solution.py
@@ -134,6 +134,7 @@
     lax.fori_loop(0, chunks, send_chunk, 0)
     in_ref[mine] = orb_ref[mine]
     dens_ref[...] = jnp.zeros_like(dens_ref)
+    ritz_ref[...] = jnp.zeros_like(ritz_ref)
 
     def all_of(ref, c, sem):
         part = ref.at[pl.ds(0, count - 1), pl.ds(2 * c, 2)]
@@ -209,7 +210,9 @@
             ritz = numerator / npw_total / (denominator / npw_total + epsilon)
             search = ((ham - ritz * orb) / (1.0 + kin)).astype(bf)
             back_ref[:, 2 * c + v] = search.reshape(in_ref.shape[0], *in_ref.shape[2:])
-            ritz_ref[c, :, v * 128 : (v + 1) * 128] = jnp.broadcast_to(ritz, (8, 128))
+            slot = lax.broadcasted_iota(jnp.int32, ritz_ref.shape, 1)
+            here = slot == mine * orb_ref.shape[1] + 2 * c + v
+            ritz_ref[...] = jnp.where(here, ritz, ritz_ref[...])
         at = pl.ds(2 * c, 2)
         out_ref[mine, at] = back_ref[mine, at]
         for k in range(1, count):
@@ -248,7 +251,7 @@
         out_specs=[whole] * 3,
         out_shape=[
             jax.ShapeDtypeStruct(orbitals.shape, jnp.bfloat16),
-            jax.ShapeDtypeStruct((chunks, 8, 256), jnp.float32),
+            jax.ShapeDtypeStruct((8, BLOCK), jnp.float32),
             jax.ShapeDtypeStruct((G, G, 2 * G), jnp.float32),
         ],
         scratch_shapes=[
@@ -269,40 +272,310 @@
     )(orbitals, potential, kin, *tabs)
 
 
-def turn_kernel(c_ref, r_ref, out_ref):
-    block = c_ref[...]
-    out_ref[0] = block
-    size = r_ref.shape[0]
-    for t in range(block.shape[1] // size):
-        at = slice(t * size, (t + 1) * size)
-        out_ref[1, :, at] = mm(block[:, at], r_ref[...]).astype(jnp.bfloat16)
-
-
-def with_turned(flat_all):
+def atom_rows(pos_ref, axis):
+    cell = lax.broadcasted_iota(jnp.int32, (G, pos_ref.shape[1]), 0)
+    shifted = (cell - pos_ref[axis : axis + 1, :] + G // 2) & (G - 1)
+    offset = (shifted - G // 2).astype(jnp.float32)
+    return jnp.exp(-offset * offset / (2.0 * sigma_cells * sigma_cells)), offset
+
+
+def split_two(values):
+    high = values.astype(jnp.bfloat16)
+    return high, (values - high.astype(jnp.float32)).astype(jnp.bfloat16)
+
+
+def quarter_turn(values, sign):
+    lane = lax.broadcasted_iota(jnp.int32, values.shape, 1)
+    first = (lane // W) % 2 == 0
+    size = values.shape[1]
+    later = pltpu.roll(values, size - W, 1)
+    earlier = pltpu.roll(values, W, 1)
+    return jnp.where(first, sign * later, -sign * earlier)
+
+
+def partial_forces(dens_ref, pos_ref, strength_ref, gy_ref, gyd_ref, f_ref):
+    atoms = pos_ref.shape[1]
+    gauss_x, offset_x = atom_rows(pos_ref, 0)
+    gauss_y, offset_y = atom_rows(pos_ref, 1)
+    gauss_z, offset_z = atom_rows(pos_ref, 2)
+    gy_ref[...] = gauss_y
+    gyd_ref[...] = gauss_y * offset_y
+    high, low = split_two(jnp.concatenate([gauss_z, gauss_z * offset_z], axis=1))
+    table = jnp.concatenate([high, high, low, jnp.zeros_like(low)], axis=0)
+    f_ref[...] = jnp.zeros_like(f_ref)
+    group = 4
+    left = lax.broadcasted_iota(jnp.int32, (G, 2 * G), 1) < G
+
+    def step(i, carry):
+        rows = []
+        for k in range(group):
+            pair = dens_ref[group * i + k]
+            both = (pair + pltpu.roll(pair, G, 1)) * (1.0 / BLOCK)
+            high_part = both.astype(jnp.bfloat16).astype(jnp.float32)
+            rest = both - high_part
+            rows.append(
+                jnp.concatenate(
+                    [jnp.where(left, high_part, rest), jnp.where(left, high_part, 0.0)], axis=1
+                ).astype(jnp.bfloat16)
+            )
+        done = mm(jnp.concatenate(rows, axis=0), table)
+        sums = [f_ref[m] for m in range(3)]
+        for k in range(group):
+            plain = done[k * G : (k + 1) * G, :atoms]
+            along = done[k * G : (k + 1) * G, atoms:]
+            at = pl.ds(group * i + k, 1)
+            gauss = gy_ref[at, :]
+            sums[0] += gauss * plain
+            sums[1] += gyd_ref[at, :] * plain
+            sums[2] += gauss * along
+        for m in range(3):
+            f_ref[m] = sums[m]
+        return carry
+
+    lax.fori_loop(0, G // group, step, 0)
+    prefactor = -strength_ref[...] / (sigma_cells * sigma_cells)
+    weights = [gauss_x * offset_x, gauss_x, gauss_x]
+    return [prefactor * jnp.sum(weights[m] * f_ref[m], axis=0, keepdims=True) for m in range(3)]
+
+
+def project_kernel(
+    c_ref, search_ref, dens_ref, ritz_in_ref, pos_ref, strength_ref,
+    out_ref, small_ref,
+    wide_ref, pair_ref, part_ref, got_ref, mid_ref, got2_ref, all_ref, proj_ref, acc_ref,
+    own_small_ref, smalls_ref, gy_ref, gyd_ref, f_ref,
+    send1, recv1, send2, recv2, send_z, recv_z, send_xy, recv_xy, send_s, recv_s,
+):
+    bf = jnp.bfloat16
+    mine, count, inner = group_place()
+    outer = count // inner
+    me_outer, me_inner = lax.axis_index(GROUP[0]), lax.axis_index(GROUP[1])
+    bands, entries = c_ref.shape
+    npw_total = W * W * W
+    lanes = 4 * W
+    blocks = entries // lanes
+    per_inner = bands // inner
+    two = 2 * BLOCK
+    per_outer = two // outer
+
+    greet_all(mine, count, inner)
+
+    def widen(i, carry):
+        size = search_ref.shape[1] * blocks
+        at = pl.ds(pl.multiple_of(i * size, size), size)
+        wide_ref[at, :] = search_ref[i].reshape(size, lanes).astype(jnp.float32)
+        return carry
+
+    lax.fori_loop(0, count, widen, 0)
+
+    def lay(j, carry):
+        block = wide_ref[pl.ds(j, BLOCK, stride=blocks), :]
+        at = pl.ds(pl.multiple_of(j * lanes, lanes), lanes)
+        pair_ref[:BLOCK, at] = block.astype(bf)
+        pair_ref[BLOCK:, at] = quarter_turn(block, 1.0).astype(bf)
+        return carry
+
+    lax.fori_loop(0, blocks, lay, 0)
+
+    depth = 1024
+
+    def overlap(quarter):
+        rows = pl.ds(pl.multiple_of(quarter * per_inner, per_inner), per_inner)
+        acc_ref[...] = jnp.zeros_like(acc_ref)
+
+        def step(i, carry):
+            at = pl.ds(pl.multiple_of(i * depth, depth), depth)
+            acc_ref[...] += lax.dot_general(
+                pair_ref[:, at], c_ref[rows, at], (((1,), (1,)), ((), ())),
+                preferred_element_type=jnp.float32,
+            )
+            return carry
+
+        lax.fori_loop(0, entries // depth, step, 0)
+
+    def to_inner(k):
+        return lax.rem(me_inner + k, inner)
+
+    def to_outer(k):
+        return lax.rem(me_outer + k, outer)
+
+    def remote(src, dst, send, recv, where):
+        return pltpu.make_async_remote_copy(
+            src_ref=src, dst_ref=dst, send_sem=send, recv_sem=recv,
+            device_id=where, device_id_type=MESH_ID,
+        )
+
+    def first_copy(k):
+        quarter = to_inner(k)
+        return remote(
+            part_ref.at[quarter], got_ref.at[me_inner], send1.at[k], recv1.at[k], {GROUP[1]: quarter}
+        )
+
+    def send_quarter(k, carry):
+        quarter = to_inner(k)
+        overlap(quarter)
+        part_ref[quarter] = (acc_ref[...] / npw_total).astype(bf)
+        first_copy(k).start()
+        return carry
+
+    lax.fori_loop(1, inner, send_quarter, 0)
+    overlap(me_inner)
+
+    forces = partial_forces(dens_ref, pos_ref, strength_ref, gy_ref, gyd_ref, f_ref)
+    own_small_ref[...] = ritz_in_ref[...]
+    for m in range(3):
+        own_small_ref[m + 1 : m + 2, :] = forces[m]
+
+    def small_copy(k):
+        peer = lax.rem(mine + k, count)
+        return remote(
+            own_small_ref, smalls_ref.at[mine], send_s.at[k], recv_s.at[k], device_of(peer, inner)
+        )
+
+    def send_small(k, carry):
+        small_copy(k).start()
+        return carry
+
+    lax.fori_loop(1, count, send_small, 0)
+    smalls_ref[mine] = own_small_ref[...]
+
+    total = acc_ref[...] / npw_total
+    for k in range(1, inner):
+        first_copy(k).wait_recv()
+        total += got_ref[lax.rem(me_inner + inner - k, inner)].astype(jnp.float32)
+    acc_ref[...] = total
+    mid_ref[...] = total.astype(bf)
+
+    def rows_of(place):
+        return pl.ds(pl.multiple_of(place * per_outer, per_outer), per_outer)
+
+    def second_copy(k):
+        place = to_outer(k)
+        return remote(
+            mid_ref.at[rows_of(place)], got2_ref.at[me_outer], send2.at[k], recv2.at[k],
+            {GROUP[0]: place},
+        )
+
+    for k in range(1, outer):
+        second_copy(k).start()
+    total = acc_ref[rows_of(me_outer), :]
+    for k in range(1, outer):
+        second_copy(k).wait_recv()
+        total += got2_ref[lax.rem(me_outer + outer - k, outer)].astype(jnp.float32)
+    all_ref[me_inner, rows_of(me_outer), :] = total.astype(bf)
+
+    own_rows = all_ref.at[me_inner, rows_of(me_outer)]
+
+    def z_copy(k):
+        return remote(own_rows, own_rows, send_z.at[k], recv_z.at[k], {GROUP[0]: to_outer(k)})
+
+    def xy_copy(place, step, k):
+        ref = all_ref.at[me_inner, rows_of(place)]
+        sem = step * inner + k
+        return remote(ref, ref, send_xy.at[sem], recv_xy.at[sem], {GROUP[1]: to_inner(k)})
+
+    for k in range(1, outer):
+        z_copy(k).start()
+    for k in range(1, inner):
+        xy_copy(me_outer, 0, k).start()
+    for step in range(1, outer):
+        z_copy(step).wait_recv()
+        place = lax.rem(me_outer + outer - step, outer)
+        for k in range(1, inner):
+            xy_copy(place, step, k).start()
+
+    width = 4 * lanes
+
+    def project(quarter, first):
+        rows = pl.ds(pl.multiple_of(quarter * per_inner, per_inner), per_inner)
+
+        def step(i, carry):
+            at = pl.ds(pl.multiple_of(i * width, width), width)
+            done = mm(all_ref[quarter], c_ref[rows, at])
+            proj_ref[:, at] = done if first else proj_ref[:, at] + done
+            return carry
+
+        lax.fori_loop(0, entries // width, step, 0)
+
+    project(me_inner, True)
+
+    def rest(k, carry):
+        quarter = lax.rem(me_inner + inner - k, inner)
+        for step in range(outer):
+            xy_copy(me_outer, step, k).wait_recv()
+        project(quarter, False)
+        return carry
+
+    lax.fori_loop(1, inner, rest, 0)
+
+    def close(j, carry):
+        at = pl.ds(pl.multiple_of(j * lanes, lanes), lanes)
+        turned = quarter_turn(proj_ref[BLOCK:, at], -1.0)
+        search = pair_ref[:BLOCK, at].astype(jnp.float32)
+        out_ref[:, at] = (search - (proj_ref[:BLOCK, at] + turned)).astype(bf)
+        return carry
+
+    lax.fori_loop(0, blocks, close, 0)
+
+    for k in range(1, count):
+        small_copy(k).wait_recv()
+    summed = smalls_ref[0]
+    for d in range(1, count):
+        summed += smalls_ref[d]
+    small_ref[...] = summed
+
+    for k in range(1, count):
+        small_copy(k).wait_send()
+    for k in range(1, inner):
+        first_copy(k).wait_send()
+        for step in range(outer):
+            xy_copy(me_outer, step, k).wait_send()
+    for k in range(1, outer):
+        second_copy(k).wait_send()
+        z_copy(k).wait_send()
+
+
+def project_all(flat_all, search, density, ritz, own_pos, strength):
+    count, inner, outer = lax.axis_size(GROUP), lax.axis_size(GROUP[1]), lax.axis_size(GROUP[0])
     bands, entries = flat_all.shape
-    one = np.zeros((2, W, 2, W), np.float32)
-    one[1, :, 0, :] = -np.eye(W)
-    one[0, :, 1, :] = np.eye(W)
-    turn = np.kron(np.eye(4, dtype=np.float32), one.reshape(2 * W, 2 * W))
-    turn = jnp.asarray(turn, dtype=jnp.bfloat16)
-    tile = 256
+    atoms = own_pos.shape[1]
+    two = 2 * BLOCK
+    whole = pl.BlockSpec(memory_space=pltpu.VMEM)
+    f32, bf = jnp.float32, jnp.bfloat16
+    sem = pltpu.SemaphoreType.DMA
     return pl.pallas_call(
-        turn_kernel,
-        grid=(bands // tile,),
-        in_specs=[
-            pl.BlockSpec((tile, entries), lambda p: (p, 0)),
-            pl.BlockSpec(turn.shape, lambda p: (0, 0)),
+        project_kernel,
+        in_specs=[whole] * 6,
+        out_specs=[whole] * 2,
+        out_shape=[
+            jax.ShapeDtypeStruct((BLOCK, entries), bf),
+            jax.ShapeDtypeStruct((8, atoms), f32),
         ],
-        out_specs=pl.BlockSpec((2, tile, entries), lambda p: (0, p, 0)),
-        out_shape=jax.ShapeDtypeStruct((2, bands, entries), jnp.bfloat16),
+        scratch_shapes=[
+            pltpu.VMEM((BLOCK * entries // (4 * W), 4 * W), f32),
+            pltpu.VMEM((two, entries), bf),
+            pltpu.VMEM((inner, two, bands // inner), bf),
+            pltpu.VMEM((inner, two, bands // inner), bf),
+            pltpu.VMEM((two, bands // inner), bf),
+            pltpu.VMEM((outer, two // outer, bands // inner), bf),
+            pltpu.VMEM((inner, two, bands // inner), bf),
+            pltpu.VMEM((two, entries), f32),
+            pltpu.VMEM((two, bands // inner), f32),
+            pltpu.VMEM((8, atoms), f32),
+            pltpu.VMEM((count, 8, atoms), f32),
+            pltpu.VMEM((G, atoms), f32),
+            pltpu.VMEM((G, atoms), f32),
+            pltpu.VMEM((3, G, atoms), f32),
+            sem((inner,)), sem((inner,)), sem((outer,)), sem((outer,)), sem((outer,)), sem((outer,)),
+            sem((inner * outer,)), sem((inner * outer,)), sem((count,)), sem((count,)),
+        ],
         compiler_params=pltpu.CompilerParams(
-            dimension_semantics=("arbitrary",), vmem_limit_bytes=40 * 1024 * 1024
+            collective_id=1, has_side_effects=True, vmem_limit_bytes=50 * 1024 * 1024
         ),
         cost_estimate=pl.CostEstimate(
-            flops=2 * bands * entries * 256, bytes_accessed=6 * bands * entries, transcendentals=0
+            flops=8 * BLOCK * bands * entries, bytes_accessed=16 << 20, transcendentals=0
         ),
-        name="with_turned",
-    )(flat_all, turn)
+        name="project_all",
+    )(flat_all, search, density, ritz, own_pos, strength)
 
 
 def wrap_offset(values):
@@ -328,20 +601,6 @@
     joined = (gauss_y[:, :, None] * gauss_z[:, None, :]).reshape(atom_count, -1)
     potential = jnp.dot((strength[:, None] * gauss_x).T, joined, precision=highest)
     return (potential, joined)
-
-
-def atom_forces(density, tables, joined, strength):
-    gauss_x, offset_x, gauss_y, offset_y, gauss_z, offset_z = tables
-    atom_count = gauss_x.shape[0]
-    with_y = ((gauss_y * offset_y)[:, :, None] * gauss_z[:, None, :]).reshape(atom_count, -1)
-    with_z = (gauss_y[:, :, None] * (gauss_z * offset_z)[:, None, :]).reshape(atom_count, -1)
-    stacked = jnp.concatenate([joined, with_y, with_z], 0)
-    moments = jnp.dot(density, stacked.T, precision=highest)
-    prefactor = -strength / (sigma_cells * sigma_cells)
-    force_x = prefactor * jnp.sum(gauss_x * offset_x * moments[:, :atom_count].T, 1)
-    force_y = prefactor * jnp.sum(gauss_x * moments[:, atom_count : 2 * atom_count].T, 1)
-    force_z = prefactor * jnp.sum(gauss_x * moments[:, 2 * atom_count :].T, 1)
-    return jnp.stack([force_x, force_y, force_z], 0)
 
 
 def chain_forces(force, own_pos, before, after):
@@ -371,7 +630,6 @@
     orbitals = jnp.einsum("ib,ik->bk", rotation[0], flat_all, preferred_element_type=jnp.float32)
     orbitals = orbitals.astype(jnp.bfloat16).reshape(BLOCK, planes * (W // 2), 4 * W)
     orbitals = orbitals.reshape(devices, vectors, planes, W // 2, 4 * W)
-    both = with_turned(flat_all)
     kind_ids = jnp.arange(SPECIES, dtype=jnp.int32)
     strength = jnp.sum(jnp.where(species[:, None] == kind_ids[None, :], depth[None, :], 0.0), 1)
     own_pos = positions[0]
@@ -380,28 +638,8 @@
     potential = jnp.swapaxes(potential.reshape(G, G, G), 0, 1)
     potential = jnp.concatenate([potential, potential], 2)
     search, ritz, density = apply_all(orbitals, potential)
-    search = search.reshape(BLOCK, -1)
-    density = jnp.swapaxes(density[:, :, :G] + density[:, :, G:], 0, 1).reshape(G, G * G) / BLOCK
-    force_part = atom_forces(density, tables, joined, strength)
-    own_ritz = ritz[:, 0, ::128].reshape(vectors)
-    ritz_part = lax.dynamic_update_slice(
-        jnp.zeros((BLOCK,), jnp.float32), own_ritz, (lax.axis_index(axes) * vectors,)
-    )
-    summed = lax.psum(jnp.concatenate([force_part.reshape(-1), ritz_part]), axes)
-    atom_force = summed[: force_part.size].reshape(force_part.shape)
-    ritz_values = summed[force_part.size :]
-    npw_total = W * W * W
-    stacked = both.reshape(2 * BANDS, -1)
-    partial = jnp.einsum("ik,jk->ij", stacked, search, preferred_element_type=jnp.float32)
-    partial = (partial / npw_total).astype(jnp.bfloat16)
-    arrived = lax.all_to_all(partial, axes, split_axis=0, concat_axis=0, tiled=True)
-    arrived = arrived.reshape(devices, 2 * BANDS // devices, BLOCK).astype(jnp.float32)
-    own_sum = jnp.sum(arrived, 0).astype(jnp.bfloat16)
-    intersections = lax.all_gather(own_sum, axes, axis=0, tiled=True)
-    projection = jnp.einsum(
-        "ij,ik->jk", intersections, stacked, preferred_element_type=jnp.float32
-    )
-    correction = (search.astype(jnp.float32) - projection).astype(jnp.bfloat16)
+    correction, small = project_all(flat_all, search, density, ritz, own_pos, strength[None])
+    ritz_values, atom_force = small[0], small[1:4]
     correction = correction.reshape(BLOCK, planes, W * 2 * W)
     image_idx = lax.axis_index("img")
     before = passed_along(own_pos, "img", 1)

time: 288 us -> 211 us (0.73); the launches traced: 283 us -> 211 us
  Pallas kernels: 109 us -> 166 us
  blocking collectives: 41.6 us -> 0 us
  matrix products: 45.5 us -> 12.1 us
  waiting for transfers between devices: 16 us -> 0.01 us
  between operations: 17.5 us -> 3.54 us
  local copies, waits for them, and re-layouts: 32.9 us -> 21.1 us
  other arithmetic: 12.5 us -> 3.33 us
  starting transfers between devices: 7.39 us -> 4.31 us
    pallas_call x1, Pallas kernels: 6.88 us -> 62.4 us  [project_all(): pl.pallas_call(project_kernel, in_specs=[whole] * 6, out_specs=[whole] *...]
    psum x1 -> x0, blocking collectives: 41.6 us -> none  [body(): lax.psum(jnp.concatenate([force_part.reshape(-1), ritz_part]), axes)]
    dot_general x3 -> x0, matrix products: 36.9 us -> none  [the longest x1 12.8 us: atom_forces(): moments = jnp.dot(density, stacked.T, precision=highest)]
    all_to_all x1 -> x0, waiting for transfers between devices: 16 us -> none  [body(): lax.all_to_all(partial, axes, split_axis=0, concat_axis=0, tiled=True)]
    mul x3 -> x0, other arithmetic: 5.22 us -> none  [the longest x1 5.11 us: local_potential(): joined = (gauss_y[:, :, None] * gauss_z[:, None, :]).reshape(atom_count, -1)]
    all_to_all x1 -> x0, starting transfers between devices: 4.76 us -> none  [body(): lax.all_to_all(partial, axes, split_axis=0, concat_axis=0, tiled=True)]
    div x2 -> x0, local copies, waits for them, and re-layouts: 4.43 us -> none  [body(): jnp.swapaxes(density[:, :, :G] + density[:, :, G:], 0, 1).reshape(G, G * G)]
    reshape x2 -> x0, local copies, waits for them, and re-layouts: 4.39 us -> none  [the longest x1 4.38 us: body(): search = search.reshape(BLOCK, -1)]
  transfers between devices with their start and end apart: 4 -> 2, of which waited for: 1 -> 0; matrix products, arithmetic and copies ran while one was open for 11% -> 14% of each run, Pallas kernels for 0% -> 79%
where the time goes in v2:
time: 211 us
  Pallas kernels  166 us (79%)
  local copies, waits for them, and re-layouts  21.1 us (10%)
  matrix products  12.1 us (6%)
  starting transfers between devices  4.31 us (2%)
  between operations  3.54 us (2%)
  other arithmetic  3.33 us (2%)
    pallas_call x1, Pallas kernels, apply_all(): pl.pallas_call(apply_kernel, in_specs=[whole] * 9, out_specs=[whole] * 3,...  104 us
    pallas_call x1, Pallas kernels, project_all(): pl.pallas_call(project_kernel, in_specs=[whole] * 6, out_specs=[whole] *...  62.4 us
    unnamed x30, local copies, waits for them, and re-layouts  17.1 us
    dot_general x1, matrix products, local_potential(): jnp.dot((strength[:, None] * gauss_x).T, joined, precision=highest)  6.15 us
    dot_general x1, matrix products, body(): jnp.einsum('ib,ik->bk', rotation[0], flat_all, preferred_element_type=jnp...  5.97 us
    ppermute x2, starting transfers between devices, passed_along(): return lax.ppermute(block, axis, route)  4.31 us
  transfers between devices with their start and end apart: 2, of which 0 were waited for; matrix products, arithmetic and copies ran while one was open for 14% of the time, Pallas kernels for 79%

profile of v2, /device:TPU:0, one launch (start us, length us, event | category | flops | bytes accessed | tf_op | source)
XLA Modules:
  0.0 210.8 jit_solution(1724252021795853338)
XLA Ops:
  0.6 0.0 copy-start
  0.6 0.7 copy.30
  1.4 1.3 collective-permute-start
  2.7 3.0 %collective-permute-start.1 = (s32[3,256]{1,0:T(4,128)S(1)}, s32[3,256]{1,0:T(4,128)S(1)}, u32[]{:S(2)}, u32[]{:S(2)}) collective-permute-start(s32[3,256]{1,0:T(4,128)S(1)} %bitcast.44), channel_id=1, source_target_pairs={{0,16},{1,17},{2,18},{3,19},{4,20},{5,21},{6,22},{7,23},{8,24},{9,... | collective-permute-start | bytes 9224 | tf_op jit(solution)/shard_map/ppermute | solution.py:28
  5.7 0.7 fusion.53
  6.4 0.1 fusion.22
  6.5 0.8 select_reduce_fusion
  7.3 6.2 %fusion.5 = f32[64,64,64]{2,1,0:T(8,128)S(1)} fusion(f32[256,64]{0,1:T(8,128)S(1)} %get-tuple-element.30, f32[256,64]{0,1:T(8,128)S(1)} %get-tuple-element.29, s32[256]{0:T(256)S(1)} %bitcast.49, f32[256]{0:T(256)S(1)} %select_reduce_fusion), kind=kOutput, calls=%fused_computation.7 | convolution fusion | flops 806666240 | bytes 1181696 | tf_op jit(solution)/shard_map/dot_general | solution.py:602
  13.5 0.6 pad_maximum_fusion.pot_ref
  14.1 12.0 %copy.21 = bf16[128,8,2,2048]{3,1,2,0:T(8,128)(2,1)} copy(bf16[128,8,2,2048]{3,2,1,0:T(2,128)(2,1)} %bitcast.48) | data formatting | bytes 16777216
  26.1 0.0 copy-done
  26.1 6.0 %fusion.8 = bf16[32,8,32,128]{3,1,2,0:T(8,128)(2,1)S(1)} fusion(bf16[1024,4096]{1,0:T(8,128)(2,1)} %bitcast.46, bf16[1,1024,256]{2,1,0:T(8,128)(2,1)S(1)} %copy-done), kind=kOutput, calls=%fused_computation.8 | convolution fusion | flops 2148532224 | bytes 11010048 | tf_op jit(solution)/shard_map/ib,ik->bk/dot_general | solution.py:630
  32.1 0.0 copy-start.1
  32.1 0.0 copy-start.2
  32.1 0.0 copy-start.3
  32.1 0.0 copy-start.4
  32.1 0.0 copy-start.5
  32.1 0.0 copy-start.6
  32.1 0.0 copy-start.7
  32.2 0.5 copy.22
  32.6 0.4 copy-done.1
  33.0 0.1 copy-done.2
  33.1 0.1 copy-done.3
  33.2 0.0 copy-done.4
  33.2 0.0 copy-done.5
  33.2 0.0 copy-done.6
  33.2 0.0 copy-done.7
  33.2 104.0 %apply_all.1 = (bf16[16,16,2,16,128]{4,3,2,1,0:T(8,128)(2,1)S(1)}, f32[8,256]{1,0:T(8,128)S(1)}, f32[64,64,128]{2,1,0:T(8,128)S(1)}) custom-call(bf16[16,16,2,16,128]{4,3,2,1,0:T(8,128)(2,1)S(1)} %bitcast.41, f32[64,64,128]{2,1,0:T(8,128)S(1)} %pad_maximum_fusion.pot_ref, f32[512,128]{1,0:T(8,128)S(1)} %copy-done.3, bf16[2,256,256]{2,1,0:T(8,128)(2,1)S(1)} %copy-done.1, ...), custom_call_target="tpu_custom_call" | custom-call | flops 3758096384 | bytes 8388608 | tf_op jit(solution)/shard_map/apply_all/pallas_call | solution.py:248
  137.2 0.0 copy-start.8
  137.2 1.3 copy-done.8
  138.5 0.0 copy-start.9
  138.5 1.4 copy-done.9
  139.8 62.4 %project_all.1 = (bf16[256,4096]{1,0:T(8,128)(2,1)S(1)}, f32[8,256]{1,0:T(8,128)S(1)}) custom-call(bf16[1024,4096]{1,0:T(8,128)(2,1)} %bitcast.47, bf16[16,16,2,16,128]{4,3,2,1,0:T(8,128)(2,1)} %copy-done.8, f32[64,64,128]{2,1,0:T(8,128)} %copy-done.9, f32[8,256]{1,0:T(8,128)S(1)} %get-tuple-element.11.ritz_in_ref, s32[3,256]{1,0:T(4,128)S(1)} %bitcast.45, ...), custom_call_target="tpu_custom_call" | custom-call | flops 8589934592 | bytes 16777216 | tf_op jit(solution)/shard_map/project_all/pallas_call | solution.py:545
  202.3 0.6 slice.21
  202.8 0.0 copy-start.10
  202.8 0.0 copy-start.11
  202.8 0.0 copy-start.12
  202.8 2.7 %broadcast_in_dim_reshape.3 = bf16[1,256,2,2048]{3,2,1,0:T(2,128)(2,1)} reshape(bf16[256,4096]{1,0:T(8,128)(2,1)S(1)} %get-tuple-element.12) | data formatting | bytes 4194304 | tf_op jit(solution)/shard_map/broadcast_in_dim;reshape | solution.py:650
  205.6 0.0 collective-permute-done
  205.6 0.0 collective-permute-done.1
  205.6 0.0 copy-done.10
  205.6 0.0 copy-done.11
  205.6 0.0 copy-done.12
  205.6 0.6 multiply_reduce_fusion.3
  206.9 0.6 multiply_reduce_fusion
  208.9 0.6 multiply_reduce_fusion.2
  210.2 0.6 copy.19
  (1 shorter events, 0.0 us)
Async XLA Ops:
  0.6 25.5 %copy-start = (bf16[1,1024,256]{2,1,0:T(8,128)(2,1)S(1)}, bf16[1,1024,256]{2,1,0:T(8,128)(2,1)}, u32[]{:S(2)}) copy-start(bf16[1,1024,256]{2,1,0:T(8,128)(2,1)} %param.15) | copy-start | bytes 1572868
  1.4 204.2 %collective-permute-start = (s32[3,256]{1,0:T(4,128)S(1)}, s32[3,256]{1,0:T(4,128)S(1)}, u32[]{:S(2)}, u32[]{:S(2)}) collective-permute-start(s32[3,256]{1,0:T(4,128)S(1)} %bitcast.43), channel_id=1, source_target_pairs={{16,0},{17,1},{18,2},{19,3},{20,4},{21,5},{22,6},{23,7},{24,8},{25... | collective-permute-start | bytes 9224 | tf_op jit(solution)/shard_map/ppermute | solution.py:28
  2.7 202.9 %collective-permute-start.1 = (s32[3,256]{1,0:T(4,128)S(1)}, s32[3,256]{1,0:T(4,128)S(1)}, u32[]{:S(2)}, u32[]{:S(2)}) collective-permute-start(s32[3,256]{1,0:T(4,128)S(1)} %bitcast.44), channel_id=1, source_target_pairs={{0,16},{1,17},{2,18},{3,19},{4,20},{5,21},{6,22},{7,23},{8,24},{9,... | collective-permute-start | bytes 9224 | tf_op jit(solution)/shard_map/ppermute | solution.py:28
  32.1 1.0 copy-start.1
  32.1 1.0 copy-start.2
  32.1 1.1 copy-start.3
  32.1 1.1 copy-start.4
  32.1 1.1 copy-start.5
  32.1 1.1 copy-start.6
  32.1 1.1 copy-start.7
  137.2 1.3 copy-start.8
  138.5 1.4 copy-start.9
  202.8 2.8 %copy-start.10 = (s32[1,3,256]{2,0,1:T(1,128)S(1)}, s32[1,3,256]{2,0,1:T(1,128)}, u32[]{:S(2)}) copy-start(s32[1,3,256]{2,0,1:T(1,128)} %param.16) | copy-start | bytes 9220
  202.8 2.8 %copy-start.11 = (s32[3,256]{1,0:T(4,128)S(1)}, s32[3,256]{1,0:T(4,128)}, u32[]{:S(2)}) copy-start(s32[3,256]{1,0:T(4,128)} %param.17) | copy-start | bytes 9220
  202.8 2.8 %copy-start.12 = (s32[3,256]{1,0:T(4,128)S(1)}, s32[3,256]{1,0:T(4,128)}, u32[]{:S(2)}) copy-start(s32[3,256]{1,0:T(4,128)} %param.18) | copy-start | bytes 9220

commit v3 on v1

v3 whole, which is shorter than its diff:
```python
import math

import jax
import jax.numpy as jnp
import numpy as np
from jax import lax
from jax.experimental import pallas as pl
from jax.experimental.pallas import tpu as pltpu
from jax.sharding import PartitionSpec as P

G = 64
W = 32
BANDS = 1024
BLOCK = 256
SPECIES = 4


kinetic_scale = 0.01
sigma_cells = 3.0
spring_constant = 2.0
epsilon = 1e-06


def phases():
    wavenum = np.arange(W, dtype=np.int32) - W // 2
    grid_cells = np.arange(G, dtype=np.int32)
    turn_count = np.mod(wavenum[:, None] * grid_cells[None, :], G)
    return turn_count.astype(np.float32) * np.float32(2.0 * math.pi / G)


def forward_table():
    angle_tab = phases()
    cosine = np.cos(angle_tab) / np.float32(math.sqrt(W))
    sine_part = np.sin(angle_tab) / np.float32(math.sqrt(W))
    return np.stack([np.stack([cosine, sine_part], 1), np.stack([-sine_part, cosine], 1)], 0)


def inverse_table():
    angle_tab = phases().T
    factor = np.float32(math.sqrt(W) / G)
    cosine = np.cos(angle_tab) * factor
    sine_part = np.sin(angle_tab) * factor
    return np.stack([np.stack([cosine, -sine_part], 1), np.stack([sine_part, cosine], 1)], 0)


def kernel_tables():
    fwd = forward_table()
    inv = inverse_table()
    two = np.eye(2, dtype=np.float32)
    table_z = np.einsum("czdn,vw,ij->jviczdwn", fwd, two, two).reshape(2, 8 * W, 4 * G)
    back_z = np.einsum("dncz,vw,ij->jdwnvicz", inv, two, two).reshape(2, 4 * G, 8 * W)
    fwd_y = fwd.reshape(2, W // 2, 2, 2, G)
    table_y = np.einsum("dgpem->empdg", fwd_y).reshape(2 * G, 2 * W)
    table_x = np.einsum("dxem->emxd", fwd).reshape(2 * G, 2 * W)
    back_x = np.einsum("emdx->xdem", inv).reshape(2 * W, 2 * G)
    inv_y = inv.reshape(2, G, 2, W // 2, 2)
    back_y = np.einsum("dmcgp->pcgdm", inv_y).reshape(2 * W, 2 * G)
    listed = (table_z, table_y, table_x, back_x, back_y, back_z)
    return [jnp.asarray(t, dtype=jnp.bfloat16) for t in listed]


def kinetic_table():
    wave = np.arange(W, dtype=np.int32) - W // 2
    sq = wave * wave
    squared = sq[:, None, None, None] + sq[None, :, None, None] + sq[None, None, None, :]
    squared = np.broadcast_to(squared, (W, W, 2, W)).reshape(W * W // 2, 4 * W)
    return np.float32(kinetic_scale * 0.5) * squared.astype(np.float32)


def mm(left, right):
    return jnp.dot(left, right, preferred_element_type=jnp.float32)


MESH_ID = pl.DeviceIdType.MESH
GROUP = ("band", "pw")
X_GROUP = 4
HALVES = 2
SPREAD = G + 8


def group_place():
    inner = lax.axis_size(GROUP[1])
    count = lax.axis_size(GROUP[0]) * inner
    mine = lax.axis_index(GROUP[0]) * inner + lax.axis_index(GROUP[1])
    return mine, count, inner


def device_of(index, inner):
    return {GROUP[0]: index // inner, GROUP[1]: lax.rem(index, inner)}


def greet_all(mine, count, inner, image, images):
    barrier = pltpu.get_barrier_semaphore()
    for k in range(1, count):
        peer = lax.rem(mine + k, count)
        pl.semaphore_signal(
            barrier, inc=1, device_id=device_of(peer, inner), device_id_type=MESH_ID
        )
    beside = sorted({1, images - 1} - {0})
    for step in beside:
        other = lax.rem(image + step, images)
        pl.semaphore_signal(barrier, inc=1, device_id={"img": other}, device_id_type=MESH_ID)
    pl.semaphore_wait(barrier, count - 1 + len(beside))


def atom_rows(pos_ref, axis):
    cell = lax.broadcasted_iota(jnp.int32, (G, pos_ref.shape[1]), 0)
    shifted = (cell - pos_ref[axis : axis + 1, :] + G // 2) & (G - 1)
    offset = (shifted - G // 2).astype(jnp.float32)
    return jnp.exp(-offset * offset / (2.0 * sigma_cells * sigma_cells)), offset


def split_two(values):
    high = values.astype(jnp.bfloat16)
    return high, (values - high.astype(jnp.float32)).astype(jnp.bfloat16)


def fill_potential(pos_ref, strength_ref, gy_ref, pot_ref):
    gauss_x = atom_rows(pos_ref, 0)[0] * strength_ref[...]
    gy_ref[...] = atom_rows(pos_ref, 1)[0]
    gauss_z = atom_rows(pos_ref, 2)[0]
    high, low = split_two(jnp.transpose(jnp.concatenate([gauss_z, gauss_z], axis=0)))
    table = jnp.concatenate([high, low], axis=1)
    group = 4

    def step(i, carry):
        rows = []
        for k in range(group):
            rows.extend(split_two(gauss_x * gy_ref[pl.ds(group * i + k, 1), :]))
        done = mm(jnp.concatenate(rows, axis=0), table)
        for k in range(group):
            top = done[2 * k * G : (2 * k + 1) * G]
            rest = done[(2 * k + 1) * G : (2 * k + 2) * G]
            pot_ref[group * i + k] = top[:, : 2 * G] + (top[:, 2 * G :] + rest[:, : 2 * G])
        return carry

    lax.fori_loop(0, G // group, step, 0)


def quarter_turn(values, sign):
    lane = lax.broadcasted_iota(jnp.int32, values.shape, 1)
    first = (lane // W) % 2 == 0
    size = values.shape[1]
    later = pltpu.roll(values, size - W, 1)
    earlier = pltpu.roll(values, W, 1)
    return jnp.where(first, sign * later, -sign * earlier)


def partial_forces(dens_ref, pos_ref, strength_ref, gy_ref, gyd_ref, f_ref):
    atoms = pos_ref.shape[1]
    gauss_x, offset_x = atom_rows(pos_ref, 0)
    gauss_y, offset_y = atom_rows(pos_ref, 1)
    gauss_z, offset_z = atom_rows(pos_ref, 2)
    gy_ref[...] = gauss_y
    gyd_ref[...] = gauss_y * offset_y
    high, low = split_two(jnp.concatenate([gauss_z, gauss_z * offset_z], axis=1))
    table = jnp.concatenate([high, high, low, jnp.zeros_like(low)], axis=0)
    f_ref[...] = jnp.zeros_like(f_ref)
    group = 4
    left = lax.broadcasted_iota(jnp.int32, (G, 2 * G), 1) < G

    def step(i, carry):
        rows = []
        for k in range(group):
            pair = dens_ref[group * i + k]
            both = (pair + pltpu.roll(pair, G, 1)) * (1.0 / BLOCK)
            high_part = both.astype(jnp.bfloat16).astype(jnp.float32)
            rest = both - high_part
            rows.append(
                jnp.concatenate(
                    [jnp.where(left, high_part, rest), jnp.where(left, high_part, 0.0)], axis=1
                ).astype(jnp.bfloat16)
            )
        done = mm(jnp.concatenate(rows, axis=0), table)
        sums = [f_ref[m] for m in range(3)]
        for k in range(group):
            plain = done[k * G : (k + 1) * G, :atoms]
            along = done[k * G : (k + 1) * G, atoms:]
            at = pl.ds(group * i + k, 1)
            gauss = gy_ref[at, :]
            sums[0] += gauss * plain
            sums[1] += gyd_ref[at, :] * plain
            sums[2] += gauss * along
        for m in range(3):
            f_ref[m] = sums[m]
        return carry

    lax.fori_loop(0, G // group, step, 0)
    prefactor = -strength_ref[...] / (sigma_cells * sigma_cells)
    weights = [gauss_x * offset_x, gauss_x, gauss_x]
    return [prefactor * jnp.sum(weights[m] * f_ref[m], axis=0, keepdims=True) for m in range(3)]


def wrap_offset(values):
    return ((values + G // 2) & (G - 1)) - G // 2


def chain_forces(force, own_pos, before, after):
    ahead_step = wrap_offset(after - own_pos).astype(jnp.float32)
    behind = wrap_offset(own_pos - before).astype(jnp.float32)
    tangent_raw = ahead_step + behind
    entries = own_pos.size

    def total(values):
        return jnp.sum(jnp.sum(values, axis=0, keepdims=True), axis=1, keepdims=True)

    def mean_square(values):
        return total(values * values) * (1.0 / entries)

    tangent = tangent_raw * (
        lax.rsqrt(mean_square(tangent_raw) + epsilon) * (1.0 / math.sqrt(entries))
    )
    length_ahead = jnp.sqrt(entries * (mean_square(ahead_step) + epsilon))
    length_behind = jnp.sqrt(entries * (mean_square(behind) + epsilon))
    along_path = total(force * tangent)
    push = spring_constant * (length_ahead - length_behind) - along_path
    return force + push * tangent, along_path


def step_kernel(
    c_hbm, orb_ref, pos_ref, strength_ref, start_ref, end_ref,
    kin_ref, tz_ref, ty_ref, tx_ref, bx_ref, by_ref, bz_ref,
    out_ref, small_ref,
    c_ref, in_ref, back_ref, search_ref, zs_ref, s_ref, pot_ref, dens_ref, gy_ref, gyd_ref, f_ref,
    wide_ref, pair_ref, part_ref, got_ref, mid_ref, got2_ref, all_ref, proj_ref, acc_ref,
    own_small_ref, smalls_ref, near_ref,
    load_sem, send_sem, recv_sem, back_send_sem, back_recv_sem,
    send1, recv1, send2, recv2, send_z, recv_z, send_xy, recv_xy, send_s, recv_s, send_n, recv_n,
):
    lanes = 2 * G
    half = W // 2
    rows = W * half
    bf = jnp.bfloat16
    mine, count, inner = group_place()
    chunks = orb_ref.shape[1] // 2

    images = lax.axis_size("img")
    image = lax.axis_index("img")
    load_c = pltpu.make_async_copy(c_hbm, c_ref, load_sem.at[0])
    load_c.start()

    def near_copy(side):
        other = lax.rem(image + (1, images - 1)[side], images)
        return pltpu.make_async_remote_copy(
            src_ref=pos_ref, dst_ref=near_ref.at[side], send_sem=send_n.at[side],
            recv_sem=recv_n.at[side], device_id={"img": other}, device_id_type=MESH_ID,
        )

    greet_all(mine, count, inner, image, images)
    if images > 1:
        for side in range(2):
            near_copy(side).start()

    def send_chunk(c, carry):
        at = pl.ds(2 * c, 2)
        for k in range(1, count):
            peer = lax.rem(mine + k, count)
            pltpu.make_async_remote_copy(
                src_ref=orb_ref.at[peer, at],
                dst_ref=in_ref.at[mine, at],
                send_sem=send_sem.at[c],
                recv_sem=recv_sem.at[c],
                device_id=device_of(peer, inner),
                device_id_type=MESH_ID,
            ).start()
        return carry

    lax.fori_loop(0, chunks, send_chunk, 0)
    in_ref[mine] = orb_ref[mine]
    dens_ref[...] = jnp.zeros_like(dens_ref)
    own_small_ref[...] = jnp.zeros_like(own_small_ref)
    fill_potential(pos_ref, strength_ref, gy_ref, pot_ref)

    def all_of(ref, c, sem):
        part = ref.at[pl.ds(0, count - 1), pl.ds(2 * c, 2)]
        return pltpu.make_async_copy(part, part, sem.at[c])

    def chunk_step(c, chunk_carry):
        all_of(in_ref, c, recv_sem).wait()
        vecs = jnp.concatenate(
            [in_ref[:, 2 * c + v].reshape(rows, 4 * W) for v in range(2)], axis=1
        )
        for p in range(2):
            zs_ref[p] = mm(vecs, tz_ref[p]).astype(bf)

        def y_step(i, carry):
            cols = []
            for k in range(2):
                at = pl.ds(pl.multiple_of((2 * i + k) * half, half), half)
                parts = [
                    zs_ref[p, at, d * lanes : (d + 1) * lanes] for p in range(2) for d in range(2)
                ]
                cols.append(jnp.concatenate(parts, axis=0))
            done = mm(ty_ref[...], jnp.concatenate(cols, axis=1))
            for k in range(2):
                for e in range(2):
                    start = pl.multiple_of((4 * i + 2 * k + e) * SPREAD, 8)
                    s_ref[pl.ds(start, G), :] = done[
                        e * G : (e + 1) * G, k * lanes : (k + 1) * lanes
                    ]
            return carry

        lax.fori_loop(0, W // 2, y_step, 0, unroll=4)

        def x_step(i, carry):
            first = 2 * X_GROUP * i
            ats = [pl.ds(first + k, 2 * W, stride=SPREAD) for k in range(2 * X_GROUP)]
            cols = [s_ref[at, :].astype(bf) for at in ats]
            for u in range(X_GROUP):
                done = mm(tx_ref[...], jnp.concatenate(cols[2 * u : 2 * u + 2], axis=1))
                real, imag = (done[:G], done[G:])
                pot = jnp.concatenate(
                    [pot_ref[first + 2 * u], pot_ref[first + 2 * u + 1]], axis=1
                )
                square = real * real + imag * imag
                for k in range(2):
                    dens_ref[first + 2 * u + k] += square[:, k * lanes : (k + 1) * lanes]
                weighted = jnp.concatenate(
                    [(real * pot).astype(bf), (imag * pot).astype(bf)], axis=0
                )
                back = mm(bx_ref[...], weighted)
                for k in range(2):
                    s_ref[ats[2 * u + k], :] = back[:, k * lanes : (k + 1) * lanes]
            return carry

        lax.fori_loop(0, G // (2 * X_GROUP), x_step, 0)

        def back_y_step(i, carry):
            cols = []
            for k in range(2):
                parts = []
                for e in range(2):
                    start = pl.multiple_of((4 * i + 2 * k + e) * SPREAD, 8)
                    parts.append(s_ref[pl.ds(start, G), :])
                cols.append(jnp.concatenate(parts, axis=0).astype(bf))
            done = mm(by_ref[...], jnp.concatenate(cols, axis=1)).astype(bf)
            for k in range(2):
                at = pl.ds(pl.multiple_of((2 * i + k) * half, half), half)
                for p in range(2):
                    for q in range(2):
                        r = (2 * p + q) * half
                        zs_ref[p, at, q * lanes : (q + 1) * lanes] = done[
                            r : r + half, k * lanes : (k + 1) * lanes
                        ]
            return carry

        lax.fori_loop(0, W // 2, back_y_step, 0, unroll=4)

        local = mm(zs_ref[0], bz_ref[0]) + mm(zs_ref[1], bz_ref[1])
        kin = kin_ref[...]
        npw_total = W * W * W
        for v in range(2):
            orb = in_ref[:, 2 * c + v].reshape(rows, 4 * W).astype(jnp.float32)
            ham = kin * orb + local[:, v * 4 * W : (v + 1) * 4 * W]
            numerator = jnp.sum(jnp.sum(orb * ham, axis=0, keepdims=True), axis=1, keepdims=True)
            denominator = jnp.sum(jnp.sum(orb * orb, axis=0, keepdims=True), axis=1, keepdims=True)
            ritz = numerator / npw_total / (denominator / npw_total + epsilon)
            search = ((ham - ritz * orb) / (1.0 + kin)).astype(bf)
            back_ref[:, 2 * c + v] = search.reshape(in_ref.shape[0], *in_ref.shape[2:])
            slot = lax.broadcasted_iota(jnp.int32, own_small_ref.shape, 1)
            here = slot == mine * orb_ref.shape[1] + 2 * c + v
            own_small_ref[...] = jnp.where(here, ritz, own_small_ref[...])
        at = pl.ds(2 * c, 2)
        search_ref[mine, at] = back_ref[mine, at]
        for k in range(1, count):
            peer = lax.rem(mine + k, count)
            pltpu.make_async_remote_copy(
                src_ref=back_ref.at[peer, at],
                dst_ref=search_ref.at[mine, at],
                send_sem=back_send_sem.at[c],
                recv_sem=back_recv_sem.at[c],
                device_id=device_of(peer, inner),
                device_id_type=MESH_ID,
            ).start()
        return chunk_carry

    lax.fori_loop(0, chunks, chunk_step, 0)

    outer = count // inner
    me_outer, me_inner = lax.axis_index(GROUP[0]), lax.axis_index(GROUP[1])
    bands, entries = c_ref.shape
    wide_lanes = 4 * W
    blocks = entries // wide_lanes
    per_inner = bands // inner
    each = orb_ref.shape[1] // HALVES
    vecs_half = BLOCK // HALVES
    two = 2 * vecs_half
    per_outer = two // outer
    spread = blocks + 8
    npw_total = W * W * W
    depth = entries // 4

    def remote(src, dst, send, recv, where):
        return pltpu.make_async_remote_copy(
            src_ref=src, dst_ref=dst, send_sem=send, recv_sem=recv,
            device_id=where, device_id_type=MESH_ID,
        )

    def to_inner(k):
        return lax.rem(me_inner + k, inner)

    def to_outer(k):
        return lax.rem(me_outer + k, outer)

    def rows_of(place):
        return pl.ds(pl.multiple_of(place * per_outer, per_outer), per_outer)

    def arrange(h):
        def wait_chunk(c, carry):
            all_of(search_ref, c, back_recv_sem).wait()
            return carry

        share = chunks // HALVES
        lax.fori_loop(h * share, (h + 1) * share, wait_chunk, 0)

        def widen(i, carry):
            for v in range(each):
                at = pl.ds(pl.multiple_of((i * each + v) * spread, 8), blocks)
                values = search_ref[i, h * each + v].reshape(blocks, wide_lanes)
                wide_ref[at, :] = values.astype(jnp.float32)
            return carry

        lax.fori_loop(0, count, widen, 0)

        def lay(j, carry):
            block = wide_ref[pl.ds(j, vecs_half, stride=spread), :]
            at = pl.ds(pl.multiple_of(j * wide_lanes, wide_lanes), wide_lanes)
            pair_ref[h, :vecs_half, at] = block.astype(bf)
            pair_ref[h, vecs_half:, at] = quarter_turn(block, 1.0).astype(bf)
            return carry

        lax.fori_loop(0, blocks, lay, 0)

    def overlap(h, quarter):
        rows = pl.ds(pl.multiple_of(quarter * per_inner, per_inner), per_inner)
        acc_ref[h] = jnp.zeros(acc_ref.shape[1:], jnp.float32)

        def step(i, carry):
            at = pl.ds(pl.multiple_of(i * depth, depth), depth)
            acc_ref[h] += lax.dot_general(
                pair_ref[h, :, at], c_ref[rows, at], (((1,), (1,)), ((), ())),
                preferred_element_type=jnp.float32,
            )
            return carry

        lax.fori_loop(0, entries // depth, step, 0)

    def first_copy(h, k):
        quarter, sem = to_inner(k), h * inner + k
        return remote(
            part_ref.at[h, quarter], got_ref.at[h, me_inner], send1.at[sem], recv1.at[sem],
            {GROUP[1]: quarter},
        )

    def overlap_all(h):
        def send_quarter(k, carry):
            quarter = to_inner(k)
            overlap(h, quarter)
            part_ref[h, quarter] = (acc_ref[h] / npw_total).astype(bf)
            first_copy(h, k).start()
            return carry

        lax.fori_loop(1, inner, send_quarter, 0)
        overlap(h, me_inner)

    def second_copy(h, k):
        place, sem = to_outer(k), h * outer + k
        return remote(
            mid_ref.at[h, rows_of(place)], got2_ref.at[h, me_outer], send2.at[sem], recv2.at[sem],
            {GROUP[0]: place},
        )

    def second_stage(h):
        total = acc_ref[h] / npw_total
        for k in range(1, inner):
            first_copy(h, k).wait_recv()
            total += got_ref[h, lax.rem(me_inner + inner - k, inner)].astype(jnp.float32)
        acc_ref[h] = total
        mid_ref[h] = total.astype(bf)
        for k in range(1, outer):
            second_copy(h, k).start()

    def z_copy(h, k):
        ref = all_ref.at[h, me_inner, rows_of(me_outer)]
        sem = h * outer + k
        return remote(ref, ref, send_z.at[sem], recv_z.at[sem], {GROUP[0]: to_outer(k)})

    def xy_copy(h, place, step, k):
        ref = all_ref.at[h, me_inner, rows_of(place)]
        sem = (h * outer + step) * inner + k
        return remote(ref, ref, send_xy.at[sem], recv_xy.at[sem], {GROUP[1]: to_inner(k)})

    def third_stage(h):
        total = acc_ref[h, rows_of(me_outer), :]
        for k in range(1, outer):
            second_copy(h, k).wait_recv()
            total += got2_ref[h, lax.rem(me_outer + outer - k, outer)].astype(jnp.float32)
        all_ref[h, me_inner, rows_of(me_outer), :] = total.astype(bf)
        for k in range(1, outer):
            z_copy(h, k).start()
        for k in range(1, inner):
            xy_copy(h, me_outer, 0, k).start()

    def forward(h):
        for step in range(1, outer):
            z_copy(h, step).wait_recv()
            place = lax.rem(me_outer + outer - step, outer)
            for k in range(1, inner):
                xy_copy(h, place, step, k).start()

    width = 4 * wide_lanes

    def project(h, quarter, first):
        rows = pl.ds(pl.multiple_of(quarter * per_inner, per_inner), per_inner)

        def step(i, carry):
            at = pl.ds(pl.multiple_of(i * width, width), width)
            done = mm(all_ref[h, quarter], c_ref[rows, at])
            proj_ref[h, :, at] = done if first else proj_ref[h, :, at] + done
            return carry

        lax.fori_loop(0, entries // width, step, 0)

    def project_rest(h):
        def rest(k, carry):
            for step in range(outer):
                xy_copy(h, me_outer, step, k).wait_recv()
            project(h, lax.rem(me_inner + inner - k, inner), False)
            return carry

        lax.fori_loop(1, inner, rest, 0)

    def small_copy(k):
        peer = lax.rem(mine + k, count)
        return remote(
            own_small_ref, smalls_ref.at[mine], send_s.at[k], recv_s.at[k], device_of(peer, inner)
        )

    def send_small(k, carry):
        small_copy(k).start()
        return carry

    load_c.wait()
    arrange(0)
    overlap_all(0)
    arrange(1)
    second_stage(0)
    overlap_all(1)
    third_stage(0)

    forces = partial_forces(dens_ref, pos_ref, strength_ref, gy_ref, gyd_ref, f_ref)
    for m in range(3):
        own_small_ref[m : m + 1, :] = forces[m]
    lax.fori_loop(1, count, send_small, 0)
    smalls_ref[mine] = own_small_ref[...]

    second_stage(1)
    forward(0)
    project(0, me_inner, True)
    third_stage(1)
    project_rest(0)
    forward(1)
    project(1, me_inner, True)

    for k in range(1, count):
        small_copy(k).wait_recv()
    summed = smalls_ref[0]
    for d in range(1, count):
        summed += smalls_ref[d]
    own = pos_ref[...]
    if images > 1:
        for side in range(2):
            near_copy(side).wait_recv()
        before = jnp.where(image == 0, start_ref[...], near_ref[0])
        after = jnp.where(image == images - 1, end_ref[...], near_ref[1])
    else:
        before, after = start_ref[...], end_ref[...]
    band, along = chain_forces(summed[:3], own, before, after)
    small_ref[...] = summed
    small_ref[:3] = band
    small_ref[4:5] = jnp.broadcast_to(along, (1, small_ref.shape[1]))

    project_rest(1)

    def close(j, carry):
        at = pl.ds(pl.multiple_of(j * wide_lanes, wide_lanes), wide_lanes)
        parts = []
        for h in range(HALVES):
            turned = quarter_turn(proj_ref[h, vecs_half:, at], -1.0)
            search = pair_ref[h, :vecs_half, at].astype(jnp.float32)
            left = search - (proj_ref[h, :vecs_half, at] + turned)
            parts.append(left.reshape(count, 1, each, wide_lanes))
        joined = jnp.concatenate(parts, axis=1).reshape(BLOCK, wide_lanes)
        out_ref[:, at] = joined.astype(bf)
        return carry

    lax.fori_loop(0, blocks, close, 0)

    def finish(c, carry):
        all_of(in_ref, c, send_sem).wait()
        all_of(search_ref, c, back_send_sem).wait()
        return carry

    lax.fori_loop(0, chunks, finish, 0)
    for k in range(1, count):
        small_copy(k).wait_send()
    for h in range(HALVES):
        for k in range(1, inner):
            first_copy(h, k).wait_send()
            for step in range(outer):
                xy_copy(h, me_outer, step, k).wait_send()
        for k in range(1, outer):
            second_copy(h, k).wait_send()
            z_copy(h, k).wait_send()
    if images > 1:
        for side in range(2):
            near_copy(side).wait_send()


def whole_step(flat_all, orbitals, own_pos, strength, start_pos, end_pos):
    devices, vectors, planes, half, lanes = orbitals.shape
    inner, outer = lax.axis_size(GROUP[1]), lax.axis_size(GROUP[0])
    bands, entries = flat_all.shape
    atoms = own_pos.shape[1]
    tabs = kernel_tables()
    kin = jnp.asarray(kinetic_table())
    whole = pl.BlockSpec(memory_space=pltpu.VMEM)
    chunks = vectors // 2
    f32, bf = jnp.float32, jnp.bfloat16
    sem, vmem = pltpu.SemaphoreType.DMA, pltpu.VMEM
    two = 2 * BLOCK // HALVES
    share = bands // inner
    flops = vectors * 2 * 2 * (W * W * 2 * W * 2 * G + W * G * 2 * W * 2 * G + G * G * 2 * W * 2 * G)
    flops += 8 * BLOCK * bands * entries
    return pl.pallas_call(
        step_kernel,
        in_specs=[pl.BlockSpec(memory_space=pltpu.HBM)] + [whole] * 12,
        out_specs=[whole] * 2,
        out_shape=[
            jax.ShapeDtypeStruct((BLOCK, entries), bf),
            jax.ShapeDtypeStruct((8, atoms), f32),
        ],
        scratch_shapes=[
            vmem((bands, entries), bf),
            vmem(orbitals.shape, bf),
            vmem(orbitals.shape, bf),
            vmem(orbitals.shape, bf),
            vmem((2, W * W // 2, 4 * G), bf),
            vmem((2 * W * SPREAD, 2 * G), f32),
            vmem((G, G, 2 * G), f32),
            vmem((G, G, 2 * G), f32),
            vmem((G, atoms), f32),
            vmem((G, atoms), f32),
            vmem((3, G, atoms), f32),
            vmem((BLOCK // HALVES * (entries // (4 * W) + 8), 4 * W), f32),
            vmem((HALVES, two, entries), bf),
            vmem((HALVES, inner, two, share), bf),
            vmem((HALVES, inner, two, share), bf),
            vmem((HALVES, two, share), bf),
            vmem((HALVES, outer, two // outer, share), bf),
            vmem((HALVES, inner, two, share), bf),
            vmem((HALVES, two, entries), f32),
            vmem((HALVES, two, share), f32),
            vmem((8, atoms), f32),
            vmem((devices, 8, atoms), f32),
            vmem((2, 3, atoms), jnp.int32),
            sem((1,)), sem((chunks,)), sem((chunks,)), sem((chunks,)), sem((chunks,)),
            sem((HALVES * inner,)), sem((HALVES * inner,)),
            sem((HALVES * outer,)), sem((HALVES * outer,)),
            sem((HALVES * outer,)), sem((HALVES * outer,)),
            sem((HALVES * inner * outer,)), sem((HALVES * inner * outer,)),
            sem((devices,)), sem((devices,)), sem((2,)), sem((2,)),
        ],
        compiler_params=pltpu.CompilerParams(
            collective_id=0, has_side_effects=True, vmem_limit_bytes=62 * 1024 * 1024
        ),
        cost_estimate=pl.CostEstimate(flops=flops, bytes_accessed=16 << 20, transcendentals=0),
        name="whole_step",
    )(flat_all, orbitals, own_pos, strength, start_pos, end_pos, kin, *tabs)


def body(coefficients, rotation, positions, start_pos, end_pos, species, depth):
    devices = lax.axis_size(GROUP)
    coeff_all = coefficients[0]
    planes = coeff_all.shape[1]
    flat_all = coeff_all.reshape(BANDS, -1)
    vectors = BLOCK // devices
    orbitals = jnp.einsum("ib,ik->bk", rotation[0], flat_all, preferred_element_type=jnp.float32)
    orbitals = orbitals.astype(jnp.bfloat16)
    orbitals = orbitals.reshape(devices, vectors, planes, W // 2, 4 * W)
    kind_ids = jnp.arange(SPECIES, dtype=jnp.int32)
    strength = jnp.sum(jnp.where(species[:, None] == kind_ids[None, :], depth[None, :], 0.0), 1)
    strength = strength[None]
    own_pos = positions[0]
    correction, small = whole_step(flat_all, orbitals, own_pos, strength, start_pos, end_pos)
    correction = correction.reshape(BLOCK, planes, W * 2 * W)
    return (correction[None], small[3:4], small[None, :3], small[4, :1])


def solution(mesh):
    in_specs = (
        P("img", None, ("band", "pw"), None),
        P("img", None, None),
        P("img", None, None),
        P(),
        P(),
        P(),
        P(),
    )
    out_specs = (
        P("img", None, ("band", "pw"), None),
        P("img", None),
        P("img", None, None),
        P("img"),
    )
    return jax.shard_map(body, mesh=mesh, in_specs=in_specs, out_specs=out_specs, check_vma=False)
```

time: 288 us -> 175 us (0.61); the launches traced: 283 us -> 174 us
  blocking collectives: 41.6 us -> 0 us
  matrix products: 45.5 us -> 5.77 us
  Pallas kernels: 109 us -> 145 us
  between operations: 17.5 us -> 0.67 us
  waiting for transfers between devices: 16 us -> 0 us
  other arithmetic: 12.5 us -> 1.4 us
  local copies, waits for them, and re-layouts: 32.9 us -> 22 us
  starting transfers between devices: 7.39 us -> 0 us
    dot_general x4 -> x0, matrix products: 43.1 us -> none  [the longest x1 12.8 us: atom_forces(): moments = jnp.dot(density, stacked.T, precision=highest)]
    psum x1 -> x0, blocking collectives: 41.6 us -> none  [body(): lax.psum(jnp.concatenate([force_part.reshape(-1), ritz_part]), axes)]
    pallas_call x2 -> x1, Pallas kernels: 109 us -> 145 us  [whole_step(): pl.pallas_call(step_kernel, in_specs=[pl.BlockSpec(memory_space=pltpu.HBM...]
    all_to_all x1 -> x0, waiting for transfers between devices: 16 us -> none  [body(): lax.all_to_all(partial, axes, split_axis=0, concat_axis=0, tiled=True)]
    mul x3 -> x0, other arithmetic: 5.22 us -> none  [the longest x1 5.11 us: local_potential(): joined = (gauss_y[:, :, None] * gauss_z[:, None, :]).reshape(atom_count, -1)]
    all_to_all x1 -> x0, starting transfers between devices: 4.76 us -> none  [body(): lax.all_to_all(partial, axes, split_axis=0, concat_axis=0, tiled=True)]
    div x2 -> x0, local copies, waits for them, and re-layouts: 4.43 us -> none  [body(): jnp.swapaxes(density[:, :, :G] + density[:, :, G:], 0, 1).reshape(G, G * G)]
    reshape x2 -> x0, local copies, waits for them, and re-layouts: 4.39 us -> none  [the longest x1 4.38 us: body(): search = search.reshape(BLOCK, -1)]
  transfers between devices with their start and end apart: 4 -> 0, of which waited for: 1 -> 0; matrix products, arithmetic and copies ran while one was open for 11% -> 0% of each run, Pallas kernels for 0% -> 0%
where the time goes in v3:
time: 175 us; the launch traced here: 174 us
  Pallas kernels  145 us (83%)
  local copies, waits for them, and re-layouts  22 us (13%)
  matrix products  5.77 us (3%)
    pallas_call x1, Pallas kernels, whole_step(): pl.pallas_call(step_kernel, in_specs=[pl.BlockSpec(memory_space=pltpu.HBM...  145 us
    unnamed x8, local copies, waits for them, and re-layouts  15.7 us
    dot_general x1, matrix products, body(): jnp.einsum('ib,ik->bk', rotation[0], flat_all, preferred_element_type=jnp...  5.77 us
    another operation x1, local copies, waits for them, and re-layouts, body(): return (correction[None], small[3:4], small[None, :3], small[4, :1])  4.47 us

profile of v3, /device:TPU:0, one launch (start us, length us, event | category | flops | bytes accessed | tf_op | source)
XLA Modules:
  0.0 174.3 jit_solution(5704800195107849629)
XLA Ops:
  0.6 0.0 copy-start
  0.6 1.4 select_reduce_fusion
  2.0 1.3 copy.24
  3.3 12.0 %copy.21 = bf16[128,8,2,2048]{3,1,2,0:T(8,128)(2,1)} copy(bf16[128,8,2,2048]{3,2,1,0:T(2,128)(2,1)} %bitcast.20) | data formatting | bytes 16777216
  15.3 0.0 copy-done
  15.3 5.8 %fusion = bf16[32,8,32,128]{3,1,2,0:T(8,128)(2,1)S(1)} fusion(bf16[1024,4096]{1,0:T(8,128)(2,1)} %bitcast.18, bf16[1,1024,256]{2,1,0:T(8,128)(2,1)S(1)} %copy-done), kind=kOutput, calls=%fused_computation.1 | convolution fusion | flops 2148532224 | bytes 11010048 | tf_op jit(solution)/shard_map/ib,ik->bk/dot_general | solution.py:688
  21.1 1.8 %copy.22 = bf16[32,8,32,128]{3,2,1,0:T(8,128)(2,1)} copy(bf16[32,8,32,128]{3,1,2,0:T(8,128)(2,1)S(1)} %fusion) | data formatting | bytes 4194304
  22.9 144.5 %whole_step.1 = (bf16[256,4096]{1,0:T(8,128)(2,1)}, f32[8,256]{1,0:T(8,128)}) custom-call(bf16[1024,4096]{1,0:T(8,128)(2,1)} %bitcast.19, bf16[16,16,2,16,128]{4,3,2,1,0:T(8,128)(2,1)} %bitcast.21, s32[3,256]{1,0:T(4,128)} %bitcast.22, f32[1,256]{1,0:T(1,128)} %bitcast.23, s32[3,256]{1,0:T(4,128)} %start_ref.1, s32[3,256]{1,0:T(4,128)} %end_ref.1, ...), custom_call_target="tpu_custom_call" | custom-call | flops 12348030976 | bytes 16777216 | tf_op jit(solution)/shard_map/whole_step/pallas_call | solution.py:635
  167.4 0.0 copy-start.1
  167.5 1.3 slice.11
  168.7 4.5 %broadcast_in_dim_reshape.3 = bf16[1,256,2,2048]{3,2,1,0:T(2,128)(2,1)} reshape(bf16[256,4096]{1,0:T(8,128)(2,1)} %get-tuple-element.6) | data formatting | bytes 4194304 | tf_op jit(solution)/shard_map/broadcast_in_dim;reshape | solution.py:697
  173.2 0.0 copy-done.1
  173.2 0.6 slice.9
  173.8 0.6 copy.19
  (1 shorter events, 0.0 us)
Async XLA Ops:
  0.6 14.7 %copy-start = (bf16[1,1024,256]{2,1,0:T(8,128)(2,1)S(1)}, bf16[1,1024,256]{2,1,0:T(8,128)(2,1)}, u32[]{:S(2)}) copy-start(bf16[1,1024,256]{2,1,0:T(8,128)(2,1)} %param.15) | copy-start | bytes 1572868
  167.4 5.7 %copy-start.1 = (f32[8,256]{1,0:T(8,128)S(1)}, f32[8,256]{1,0:T(8,128)}, u32[]{:S(2)}) copy-start(f32[8,256]{1,0:T(8,128)} %get-tuple-element.7) | copy-start | bytes 24580

commit v4 on v3

--- a/solution.py
+++ b/solution.py
@@ -672,7 +672,7 @@
             sem((devices,)), sem((devices,)), sem((2,)), sem((2,)),
         ],
         compiler_params=pltpu.CompilerParams(
-            collective_id=0, has_side_effects=True, vmem_limit_bytes=62 * 1024 * 1024
+            collective_id=0, has_side_effects=True, vmem_limit_bytes=48 * 1024 * 1024
         ),
         cost_estimate=pl.CostEstimate(flops=flops, bytes_accessed=16 << 20, transcendentals=0),
         name="whole_step",

time: 175 us -> 167 us (0.954)
  Pallas kernels: 145 us -> 141 us
  local copies, waits for them, and re-layouts: 22 us -> 18.2 us
    pallas_call x1, Pallas kernels: 145 us -> 141 us  [whole_step(): pl.pallas_call(step_kernel, in_specs=[pl.BlockSpec(memory_space=pltpu.HBM...]
    unnamed x8 -> x24, local copies, waits for them, and re-layouts: 15.7 us -> 14.4 us
where the time goes in v4:
time: 167 us
  Pallas kernels  141 us (84%)
  local copies, waits for them, and re-layouts  18.2 us (11%)
  matrix products  5.77 us (3%)
    pallas_call x1, Pallas kernels, whole_step(): pl.pallas_call(step_kernel, in_specs=[pl.BlockSpec(memory_space=pltpu.HBM...  141 us
    unnamed x24, local copies, waits for them, and re-layouts  14.4 us
    dot_general x1, matrix products, body(): jnp.einsum('ib,ik->bk', rotation[0], flat_all, preferred_element_type=jnp...  5.77 us

profile of v4, /device:TPU:0, one launch (start us, length us, event | category | flops | bytes accessed | tf_op | source)
XLA Modules:
  0.0 167.0 jit_solution(755445137008010860)
XLA Ops:
  0.6 0.0 copy-start
  0.6 0.8 select_reduce_fusion
  1.5 0.7 copy.24
  2.2 12.0 %copy.21 = bf16[128,8,2,2048]{3,1,2,0:T(8,128)(2,1)} copy(bf16[128,8,2,2048]{3,2,1,0:T(2,128)(2,1)} %bitcast.23) | data formatting | bytes 16777216
  14.2 0.0 copy-done
  14.2 5.8 %fusion = bf16[32,8,32,128]{3,1,2,0:T(8,128)(2,1)S(1)} fusion(bf16[1024,4096]{1,0:T(8,128)(2,1)} %bitcast.21, bf16[1,1024,256]{2,1,0:T(8,128)(2,1)S(1)} %copy-done), kind=kOutput, calls=%fused_computation.1 | convolution fusion | flops 2148532224 | bytes 11010048 | tf_op jit(solution)/shard_map/ib,ik->bk/dot_general | solution.py:688
  20.0 0.0 copy-start.1
  20.0 0.0 copy-start.2
  20.0 0.0 copy-start.3
  20.0 0.0 copy-start.4
  20.0 0.0 copy-start.5
  20.0 0.0 copy-start.6
  20.0 0.0 copy-start.7
  20.1 0.0 copy-start.8
  20.1 0.0 copy-start.9
  20.1 0.5 copy.22
  20.6 0.1 copy-done.1
  20.7 0.0 copy-done.2
  20.7 0.3 copy-done.3
  21.0 0.1 copy-done.4
  21.0 0.1 copy-done.5
  21.1 0.0 copy-done.6
  21.1 0.0 copy-done.7
  21.1 0.0 copy-done.8
  21.1 0.0 copy-done.9
  21.1 141.4 %whole_step.1 = (bf16[256,4096]{1,0:T(8,128)(2,1)S(1)}, f32[8,256]{1,0:T(8,128)S(1)}) custom-call(bf16[1024,4096]{1,0:T(8,128)(2,1)} %bitcast.22, bf16[16,16,2,16,128]{4,3,2,1,0:T(8,128)(2,1)S(1)} %bitcast.18, s32[3,256]{1,0:T(4,128)S(1)} %bitcast.19, f32[1,256]{1,0:T(1,128)S(1)} %bitcast.20, s32[3,256]{1,0:T(4,128)S(1)} %copy-done.1, ...), custom_call_target="tpu_custom_call" | custom-call | flops 12348030976 | bytes 16777216 | tf_op jit(solution)/shard_map/whole_step/pallas_call | solution.py:635
  162.6 0.5 slice.11
  163.1 2.7 %broadcast_in_dim_reshape.3 = bf16[1,256,2,2048]{3,2,1,0:T(2,128)(2,1)} reshape(bf16[256,4096]{1,0:T(8,128)(2,1)S(1)} %get-tuple-element.6) | data formatting | bytes 4194304 | tf_op jit(solution)/shard_map/broadcast_in_dim;reshape | solution.py:697
  165.8 0.6 slice.9
  166.4 0.6 copy.19
  (1 shorter events, 0.0 us)
Async XLA Ops:
  0.6 13.6 %copy-start = (bf16[1,1024,256]{2,1,0:T(8,128)(2,1)S(1)}, bf16[1,1024,256]{2,1,0:T(8,128)(2,1)}, u32[]{:S(2)}) copy-start(bf16[1,1024,256]{2,1,0:T(8,128)(2,1)} %param.15) | copy-start | bytes 1572868
  20.0 0.7 copy-start.1
  20.0 0.7 copy-start.2
  20.0 1.0 copy-start.3
  20.0 1.0 copy-start.4
  20.0 1.1 copy-start.5
  20.0 1.1 copy-start.6
  20.0 1.1 copy-start.7
  20.1 1.1 copy-start.8
  20.1 1.1 copy-start.9
